TPU v7x, 32 devices: a whole 2x2x4 slice. The times are simulated.
32 devices in a mesh: rep: 2 (over x), dp: 16 (over y, z, core).
Axes of the slice: x: 2, y: 2, z: 4, core: 2. Of those that a mesh axis runs over, the one named last changes fastest.
Arguments:
- x: bfloat16 [32, 2048, 1024], P(('rep', 'dp')), parts along dimension 0
- dy: bfloat16 [32, 2048, 1024], P(('rep', 'dp')), parts along dimension 0
- w_gate: bfloat16 [2, 1024, 3200], replicated
- w_up: bfloat16 [2, 1024, 3200], replicated
- w_down: bfloat16 [2, 3200, 1024], replicated
- m_w_gate: float32 [2, 1024, 3200], P(None, 'dp')
- m_w_up: float32 [2, 1024, 3200], P(None, 'dp')
- m_w_down: float32 [2, 3200, 1024], P(None, 'dp')
- v_w_gate: float32 [2, 1024, 3200], P(None, 'dp')
- v_w_up: float32 [2, 1024, 3200], P(None, 'dp')
- v_w_down: float32 [2, 3200, 1024], P(None, 'dp')
Outputs:
- output 1: bfloat16 [4, 1024, 3200], P('rep'), parts along dimension 0
- output 2: bfloat16 [4, 1024, 3200], P('rep'), parts along dimension 0
- output 3: bfloat16 [4, 3200, 1024], P('rep'), parts along dimension 0
- output 4: float32 [4, 1024, 3200], P('rep', 'dp'), parts along dimension 0
- output 5: float32 [4, 1024, 3200], P('rep', 'dp'), parts along dimension 0
- output 6: float32 [4, 3200, 1024], P('rep', 'dp'), parts along dimension 0
- output 7: float32 [4, 1024, 3200], P('rep', 'dp'), parts along dimension 0
- output 8: float32 [4, 1024, 3200], P('rep', 'dp'), parts along dimension 0
- output 9: float32 [4, 3200, 1024], P('rep', 'dp'), parts along dimension 0
There are 2 independent parts. A program takes and returns all parts, laid end to end along the dimension named above; an argument that names none is the same for every part.
All inputs are finite; a program needn't handle non-finite values.
Results may differ from a plain program's by a relative error of at most 0.022.
Values are sent between devices in bfloat16 or wider.
A program may use at most 2 GiB of HBM per device.

v0:
```python
import jax
import jax.numpy as jnp
from jax import lax

NAMES = ("w_gate", "w_up", "w_down")


def matmul(a, w):
    return jnp.dot(a, w, preferred_element_type=jnp.float32).astype(jnp.bfloat16)


def normed(h):
    wide = h.astype(jnp.float32)
    scale = lax.rsqrt(jnp.mean(wide**2, -1, keepdims=True) + 1e-6)
    return (wide * scale).astype(jnp.bfloat16)


def layer(h, w):
    a = normed(h)
    gate = jnp.dot(a, w["w_gate"], preferred_element_type=jnp.float32)
    up = jnp.dot(a, w["w_up"], preferred_element_type=jnp.float32)
    return h + matmul((jax.nn.silu(gate) * up).astype(jnp.bfloat16), w["w_down"])


def adamw(w, m, v, g):
    m = 0.9 * m + 0.1 * g
    v = 0.95 * v + 0.05 * g * g
    step = m * lax.rsqrt(v + 1e-8) + 0.1 * w
    return (w - 0.02 * step).astype(jnp.bfloat16), m, v


def clipped(gradients, sum_of_squares, count):
    factor = jnp.minimum(1.0, 0.5 * lax.rsqrt(sum_of_squares / count + 1e-30))
    return [g * factor for g in gradients]


def stack(weights, h):
    for number in range(weights["w_gate"].shape[0]):
        h = layer(h, {name: w[number] for name, w in weights.items()})
    return h


def solution(mesh):
    groups = mesh.shape["rep"]

    def step(x, dy, *arrays):
        weights, m, v = (arrays[i : i + 3] for i in (0, 3, 6))
        x, dy = (t.reshape(groups, -1, *t.shape[1:]) for t in (x, dy))

        def of_a_group(x, dy):
            _, back = jax.vjp(lambda w: stack(w, x), dict(zip(NAMES, weights, strict=True)))
            by_weights = back(dy)[0]
            gradients = [by_weights[name].astype(jnp.float32) for name in NAMES]
            gradients = clipped(gradients, sum(jnp.sum(g * g) for g in gradients), sum(g.size for g in gradients))
            new = [adamw(w.astype(jnp.float32), m, v, g) for w, m, v, g in zip(weights, m, v, gradients, strict=True)]
            return tuple(one[which] for which in range(3) for one in new)

        return tuple(t.reshape(-1, *t.shape[2:]) for t in jax.vmap(of_a_group)(x, dy))

    return step
```

profile of v0, /device:TPU:0, one launch (start us, length us, event | category | flops | bytes accessed | tf_op | source)
XLA Modules:
  0.0 1873.0 jit_solution(3309803914035476865)
XLA Ops:
  22.6 20.9 %fusion.188 = f32[2048,3200]{1,0:T(8,128)} fusion(bf16[2,1024,3200]{2,1,0:T(8,128)(2,1)} %param.12, bf16[1,2048,1024]{2,1,0:T(8,128)(2,1)S(1)} %copy-done.14, f32[2048]{0:T(1024)S(1)} %add_rsqrt_fusion), kind=kOutput, calls=%fused_computation.228 | convolution fusion | flops 13428064256 | bytes 36970496 | tf_op jit(solution)/vmap(jvp())/dot_general | solution.py:20
  43.5 32.1 %fusion.164 = (bf16[1,1,2048,3200]{3,2,1,0:T(8,128)(2,1)}, f32[2048,3200]{1,0:T(8,128)}) fusion(f32[2048,3200]{1,0:T(8,128)} %fusion.188, bf16[2,1024,3200]{2,1,0:T(8,128)(2,1)} %param.15, bf16[1,2048,1024]{2,1,0:T(8,128)(2,1)} %param.14, f32[2048]{0:T(1024)S(1)} %add_rsqrt_fusion), kind=kOutput, calls=%fused_computation.191 | convolution fusion | flops 13467385856 | bytes 76292096 | tf_op jit(solution)/vmap(jvp())/dot_general | solution.py:21
  75.5 22.1 %fusion.174 = (f32[2048]{0:T(1024)S(1)}, bf16[1,1,2048,1024]{2,3,1,0:T(8,128)(2,1)}) fusion(bf16[2,3200,1024]{2,1,0:T(8,128)(2,1)} %param.16, bf16[1,1,2048,3200]{3,2,1,0:T(8,128)(2,1)} %get-tuple-element.263, bf16[1,2048,1024]{1,2,0:T(8,128)(2,1)} %copy), kind=kOutput, calls=%fused_computation.213 | convolution fusion | flops 13432256512 | bytes 28057600 | tf_op jit(solution)/vmap(jvp())/dot_general | solution.py:9
  101.5 22.3 %fusion.177 = f32[2048,3200]{1,0:T(8,128)} fusion(bf16[2,1024,3200]{2,1,0:T(8,128)(2,1)} %param.12, bf16[1,1,2048,1024]{2,3,1,0:T(8,128)(2,1)S(1)} %fusion.175), kind=kOutput, calls=%fused_computation.217 | convolution fusion | flops 13421772800 | bytes 36962304 | tf_op jit(solution)/vmap(jvp())/dot_general | solution.py:20
  123.8 30.0 %fusion.163 = (bf16[1,1,2048,3200]{3,2,1,0:T(8,128)(2,1)}, f32[2048,3200]{1,0:T(8,128)}) fusion(f32[2048,3200]{1,0:T(8,128)} %fusion.177, bf16[2,1024,3200]{2,1,0:T(8,128)(2,1)} %param.15, bf16[1,1,2048,1024]{2,3,1,0:T(8,128)(2,1)S(1)} %fusion.175), kind=kOutput, calls=%fused_computation.189 | convolution fusion | flops 13461094400 | bytes 76283904 | tf_op jit(solution)/vmap(jvp())/dot_general | solution.py:21
  160.3 39.2 %convert_multiply_fusion.2 = (bf16[1,1,2048,3200]{3,2,1,0:T(8,128)(2,1)}, bf16[1,1,2048,3200]{3,2,1,0:T(8,128)(2,1)}) fusion(f32[2048,3200]{1,0:T(8,128)} %fusion.177, f32[2048,3200]{1,0:T(8,128)} %get-tuple-element.270, bf16[2,3200,1024]{2,1,0:T(8,128)(2,1)} %param.16, bf16[1,2048,1024]{2,1,0:T(8,128)(2,1)} %param.17), kind=kOutput, calls=%fused_computation.172 | convolution fusion | flops 13526630400 | bytes 89391104 | tf_op jit(solution)/vmap(transpose(jvp()))/dot_general | solution.py:9
  199.5 19.9 %fusion.156 = bf16[2048,1024]{0,1:T(8,128)(2,1)} fusion(bf16[1,1,2048,3200]{3,2,1,0:T(8,128)(2,1)} %get-tuple-element.545, bf16[2,1024,3200]{2,1,0:T(8,128)(2,1)} %param.12), kind=kOutput, calls=%fused_computation.178 | convolution fusion | flops 13421772800 | bytes 23855104 | tf_op jit(solution)/vmap(transpose(jvp()))/dot_general | solution.py:20
  219.4 21.5 %fusion.176 = (f32[2048]{0:T(1024)S(1)}, bf16[2048,1024]{0,1:T(8,128)(2,1)}) fusion(bf16[1,1,2048,1024]{2,3,1,0:T(8,128)(2,1)S(1)} %copy-done.12, bf16[2048,1024]{0,1:T(8,128)(2,1)} %fusion.156, bf16[2,1024,3200]{2,1,0:T(8,128)(2,1)} %param.15, bf16[1,1,2048,3200]{3,2,1,0:T(8,128)(2,1)} %get-tuple-element.623), kind=kOutput, calls=%fused_computation.215 | convolution fusion | flops 13432256512 | bytes 32251904 | tf_op jit(solution)/vmap(transpose(jvp()))/dot_general | solution.py:21
  247.4 36.5 %convert_multiply_fusion = (bf16[1,1,2048,3200]{3,2,1,0:T(8,128)(2,1)}, bf16[1,1,2048,3200]{3,2,1,0:T(8,128)(2,1)}) fusion(f32[2048,3200]{1,0:T(8,128)} %fusion.188, f32[2048,3200]{1,0:T(8,128)} %get-tuple-element.264, bf16[2,3200,1024]{2,1,0:T(8,128)(2,1)} %param.16, bf16[1,1,2048,1024]{2,3,1,0:T(8,128)(2,1)S(1)} %fusion.199), kind=kOutput, calls=%fused_computation.170 | convolution fusion | flops 13526630400 | bytes 89391104 | tf_op jit(solution)/vmap(transpose(jvp()))/dot_general | solution.py:9
  283.9 165.4 %while.13 = (bf16[1,1,2048,1024]{2,3,1,0:T(8,128)(2,1)}, bf16[1,1,2048,3200]{3,2,1,0:T(8,128)(2,1)}, f32[1,64,3200]{2,1,0:T(8,128)S(1)}, f32[1,64,3200]{2,1,0:T(...) while((bf16[1,1,2048,1024]{2,3,1,0:T(8,128)(2,1)}, ...), condition=%wide.windowed_dot_general_cond_rs.1.clone, body=%wide.windowed_dot_general_body_rs.1.clone.sunk | while | flops 3358769152 | bytes 120193760 | solution.py:20
  312.4 14.1 collective-permute-done.6
  355.8 13.1 collective-permute-done.6
  396.0 9.3 collective-permute-done.6
  422.1 7.0 collective-permute-done.5
  436.1 8.0 collective-permute-done.6
  452.7 191.8 %while.12 = (bf16[1,1,2048,1024]{2,3,1,0:T(8,128)(2,1)}, bf16[1,1,2048,3200]{3,2,1,0:T(8,128)(2,1)}, f32[1,64,3200]{2,1,0:T(8,128)S(1)}, f32[1,64,3200]{2,1,0:T(...) while((bf16[1,1,2048,1024]{2,3,1,0:T(8,128)(2,1)}, ...), condition=%wide.windowed_dot_general_cond_rs.clone, body=%wide.windowed_dot_general_body_rs.clone.sunk | while | flops 3358769152 | bytes 120193760 | solution.py:20
  468.0 11.1 collective-permute-done
  485.9 8.0 collective-permute-done.2
  502.5 7.5 collective-permute-start
  535.0 16.0 collective-permute-done.2
  568.3 7.5 collective-permute-done
  582.6 13.4 collective-permute-done.2
  627.3 16.2 collective-permute-done.2
  645.4 192.5 %while.15 = (bf16[1,1,2048,1024]{2,3,1,0:T(8,128)(2,1)}, bf16[1,1,2048,3200]{3,2,1,0:T(8,128)(2,1)}, f32[1,64,3200]{2,1,0:T(8,128)S(1)}, f32[1,64,3200]{2,1,0:T(...) while((bf16[1,1,2048,1024]{2,3,1,0:T(8,128)(2,1)}, ...), condition=%wide.windowed_dot_general_cond_rs.3.clone, body=%wide.windowed_dot_general_body_rs.3.clone.sunk | while | flops 3358769152 | bytes 120193760 | solution.py:21
  660.7 15.9 collective-permute-done.12
  683.3 15.9 collective-permute-done.14
  716.7 7.2 collective-permute-done.12
  730.7 15.6 collective-permute-done.14
  756.8 7.0 fusion.330
  775.6 12.7 collective-permute-done.14
  820.8 16.1 collective-permute-done.14
  838.0 17.5 copy.4
  861.9 18.2 copy.2
  886.5 185.5 %while.14 = (bf16[1,1,2048,1024]{2,3,1,0:T(8,128)(2,1)}, bf16[1,1,2048,3200]{3,2,1,0:T(8,128)(2,1)}, f32[1,64,3200]{2,1,0:T(8,128)S(1)}, f32[1,64,3200]{2,1,0:T(...) while((bf16[1,1,2048,1024]{2,3,1,0:T(8,128)(2,1)}, ...), condition=%wide.windowed_dot_general_cond_rs.2.clone, body=%wide.windowed_dot_general_body_rs.2.clone.sunk | while | flops 3358769152 | bytes 120193760 | solution.py:21
  915.9 16.8 collective-permute-done.10
  943.8 7.0 fusion.322
  964.2 16.3 collective-permute-done.10
  998.6 7.4 collective-permute-done.8
  1012.7 13.2 collective-permute-done.10
  1055.6 15.3 collective-permute-done.10
  1072.0 187.1 %while.17 = (bf16[1,1,2048,3200]{2,3,1,0:T(8,128)(2,1)}, bf16[1,1,2048,1024]{3,2,1,0:T(8,128)(2,1)}, f32[1,200,1024]{2,1,0:T(8,128)S(1)}, f32[1,200,1024]{2,1,0:...) while((bf16[1,1,2048,3200]{2,3,1,0:T(8,128)(2,1)}, ...), condition=%wide.windowed_dot_general_cond_rs.5.clone, body=%wide.windowed_dot_general_body_rs.5.clone.sunk | while | flops 3363225600 | bytes 64094820 | solution.py:9
  1085.0 8.3 collective-permute-done.20
  1105.3 12.0 collective-permute-done.22
  1133.7 8.0 collective-permute-done.20
  1153.6 10.9 collective-permute-done.22
  1181.0 7.7 collective-permute-done.20
  1200.7 10.0 collective-permute-done.22
  1227.1 7.7 collective-permute-done.20
  1246.8 10.0 collective-permute-done.22
  1259.2 189.4 %while.16 = (bf16[1,1,2048,3200]{2,3,1,0:T(8,128)(2,1)}, bf16[1,1,2048,1024]{3,2,1,0:T(8,128)(2,1)}, f32[1,200,1024]{2,1,0:T(8,128)S(1)}, f32[1,200,1024]{2,1,0:...) while((bf16[1,1,2048,3200]{2,3,1,0:T(8,128)(2,1)}, ...), condition=%wide.windowed_dot_general_cond_rs.4.clone, body=%wide.windowed_dot_general_body_rs.4.clone.sunk | while | flops 3363225600 | bytes 64094820 | solution.py:9
  1272.2 8.4 collective-permute-done.16
  1292.8 9.6 collective-permute-done.18
  1319.0 9.5 collective-permute-done.16
  1340.7 9.4 collective-permute-done.18
  1366.7 10.2 collective-permute-done.16
  1389.1 10.1 collective-permute-done.18
  1415.8 8.8 collective-permute-done.16
  1436.8 9.1 collective-permute-done.18
  1473.0 7.5 collective-permute-done.28
  1483.5 30.6 %all-reduce.10 = f32[1]{0:T(128)} all-reduce(f32[1]{0:T(128)} %bitcast.39), channel_id=13, replica_groups=mesh['rep'=2,'dp'=16] {'dp'}, use_global_device_ids=true, to_apply=%region_3.4.clone | all-reduce | flops 1 | bytes 8 | tf_op jit(solution)/vmap()/reduce_sum | solution.py:54
  1530.3 100.1 %all-gather.10.cloned.1.call-done = bf16[1,2,1024,3200]{3,2,1,0:T(8,128)(2,1)} async-done(((bf16[1,2,64,3200]{3,2,1,0:T(8,128)(2,1)}), bf16[1,2,1024,3200]{3,2,1,0:T(8,128)(2,1)}) %all-gather.10.cloned.1.call-update) | async-done | bytes 13107216 | tf_op jit(solution)/reshape | solution.py:58
  1630.4 104.6 %all-gather.12.cloned.1.call-done = bf16[1,2,1024,3200]{3,2,1,0:T(8,128)(2,1)} async-done(((bf16[1,2,64,3200]{3,2,1,0:T(8,128)(2,1)}), bf16[1,2,1024,3200]{3,2,1,0:T(8,128)(2,1)}) %all-gather.12.cloned.1.call-update) | async-done | bytes 13107216 | tf_op jit(solution)/reshape | solution.py:58
  1735.0 104.6 %all-gather.14.cloned.1.call-done = bf16[1,2,3200,1024]{3,2,1,0:T(8,128)(2,1)} async-done(((bf16[1,2,200,1024]{3,2,1,0:T(8,128)(2,1)}), bf16[1,2,3200,1024]{3,2,1,0:T(8,128)(2,1)}) %all-gather.14.cloned.1.call-update) | async-done | bytes 13107216 | tf_op jit(solution)/reshape | solution.py:58
  1839.6 12.7 copy.63
  (606 shorter events, 718.5 us)
Async XLA Ops:
  7.2 1623.2 %all-gather.10.cloned.1.call-start = ((), (), s32[]{:S(2)}) async-start(), calls=%async_computation | async-start | bytes 13926400 | tf_op jit(solution)/reshape | solution.py:58
  284.0 21.7 %collective-permute-start.4 = (f32[1,64,3200]{2,1,0:T(8,128)S(1)}, f32[1,64,3200]{2,1,0:T(8,128)S(1)}, u32[]{:S(2)}, u32[]{:S(2)}) collective-permute-start(f32[1,64,3200]{2,1,0:T(8,128)S(1)} %broadcast_select_fusion.26), channel_id=9, source_target_pairs={{0,1},{1,2},{2,3},{3,4},{4,5},{5,6},{6,7},{7,8},{8,9},{9,10},{10,1... | collective-permute-start | bytes 2457608 | tf_op jit(solution)/vmap(transpose(jvp()))/dot_general | solution.py:20
  284.7 21.0 %collective-permute-start.5 = (f32[1,64,3200]{2,1,0:T(8,128)S(1)}, f32[1,64,3200]{2,1,0:T(8,128)S(1)}, u32[]{:S(2)}, u32[]{:S(2)}) collective-permute-start(f32[1,64,3200]{2,1,0:T(8,128)S(1)} %broadcast_select_fusion.27), channel_id=8, source_target_pairs={{0,15},{1,0},{2,1},{3,2},{4,3},{5,4},{6,5},{7,6},{8,7},{9,8},{10,9... | collective-permute-start | bytes 2457608 | tf_op jit(solution)/vmap(transpose(jvp()))/dot_general | solution.py:20
  305.9 20.6 %collective-permute-start.6 = (f32[1,64,3200]{2,1,0:T(8,128)S(1)}, f32[1,64,3200]{2,1,0:T(8,128)S(1)}, u32[]{:S(2)}, u32[]{:S(2)}) collective-permute-start(f32[1,64,3200]{2,1,0:T(8,128)S(1)} %get-tuple-element.465), channel_id=11, source_target_pairs={{0,1},{1,2},{2,3},{3,4},{4,5},{5,6},{6,7},{7,8},{8,9},{9,10},{10,1... | collective-permute-start | bytes 2457608 | tf_op jit(solution)/vmap(transpose(jvp()))/dot_general | solution.py:20
  328.8 20.2 %collective-permute-start.4 = (f32[1,64,3200]{2,1,0:T(8,128)S(1)}, f32[1,64,3200]{2,1,0:T(8,128)S(1)}, u32[]{:S(2)}, u32[]{:S(2)}) collective-permute-start(f32[1,64,3200]{2,1,0:T(8,128)S(1)} %broadcast_select_fusion.26), channel_id=9, source_target_pairs={{0,1},{1,2},{2,3},{3,4},{4,5},{5,6},{6,7},{7,8},{8,9},{9,10},{10,1... | collective-permute-start | bytes 2457608 | tf_op jit(solution)/vmap(transpose(jvp()))/dot_general | solution.py:20
  328.9 20.1 %collective-permute-start.5 = (f32[1,64,3200]{2,1,0:T(8,128)S(1)}, f32[1,64,3200]{2,1,0:T(8,128)S(1)}, u32[]{:S(2)}, u32[]{:S(2)}) collective-permute-start(f32[1,64,3200]{2,1,0:T(8,128)S(1)} %broadcast_select_fusion.27), channel_id=8, source_target_pairs={{0,15},{1,0},{2,1},{3,2},{4,3},{5,4},{6,5},{7,6},{8,7},{9,8},{10,9... | collective-permute-start | bytes 2457608 | tf_op jit(solution)/vmap(transpose(jvp()))/dot_general | solution.py:20
  449.3 1000.5 %collective-permute-start.25 = (f32[1,64,3200]{2,1,0:T(8,128)}, f32[1,64,3200]{2,1,0:T(8,128)}, u32[]{:S(2)}, u32[]{:S(2)}) collective-permute-start(f32[1,64,3200]{2,1,0:T(8,128)} %get-tuple-element.39), channel_id=12, source_target_pairs={{0,1},{1,2},{2,3},{3,4},{4,5},{5,6},{6,7},{7,8},{8,9},{9,10},{10,1... | collective-permute-start | bytes 2457608 | tf_op jit(solution)/vmap(transpose(jvp()))/dot_general | solution.py:20
  453.0 26.1 %collective-permute-start = (f32[1,64,3200]{2,1,0:T(8,128)S(1)}, f32[1,64,3200]{2,1,0:T(8,128)S(1)}, u32[]{:S(2)}, u32[]{:S(2)}) collective-permute-start(f32[1,64,3200]{2,1,0:T(8,128)S(1)} %broadcast_select_fusion.24), channel_id=3, source_target_pairs={{0,1},{1,2},{2,3},{3,4},{4,5},{5,6},{6,7},{7,8},{8,9},{9,10},{10,1... | collective-permute-start | bytes 2457608 | tf_op jit(solution)/vmap(transpose(jvp()))/dot_general | solution.py:20
  454.9 24.3 %collective-permute-start.1 = (f32[1,64,3200]{2,1,0:T(8,128)}, f32[1,64,3200]{2,1,0:T(8,128)S(1)}, u32[]{:S(2)}, u32[]{:S(2)}) collective-permute-start(f32[1,64,3200]{2,1,0:T(8,128)} %broadcast_select_fusion.25), channel_id=2, source_target_pairs={{0,15},{1,0},{2,1},{3,2},{4,3},{5,4},{6,5},{7,6},{8,7},{9,8},{10,9... | collective-permute-start | bytes 2457608 | tf_op jit(solution)/vmap(transpose(jvp()))/dot_general | solution.py:20
  479.8 20.4 %collective-permute-start.3 = (f32[1,64,3200]{2,1,0:T(8,128)S(1)}, f32[1,64,3200]{2,1,0:T(8,128)S(1)}, u32[]{:S(2)}, u32[]{:S(2)}) collective-permute-start(f32[1,64,3200]{2,1,0:T(8,128)S(1)} %get-tuple-element.457), channel_id=4, source_target_pairs={{0,15},{1,0},{2,1},{3,2},{4,3},{5,4},{6,5},{7,6},{8,7},{9,8},{10,9... | collective-permute-start | bytes 2457608 | tf_op jit(solution)/vmap(transpose(jvp()))/dot_general | solution.py:20
  502.5 21.9 %collective-permute-start = (f32[1,64,3200]{2,1,0:T(8,128)S(1)}, f32[1,64,3200]{2,1,0:T(8,128)S(1)}, u32[]{:S(2)}, u32[]{:S(2)}) collective-permute-start(f32[1,64,3200]{2,1,0:T(8,128)S(1)} %broadcast_select_fusion.24), channel_id=3, source_target_pairs={{0,1},{1,2},{2,3},{3,4},{4,5},{5,6},{6,7},{7,8},{8,9},{9,10},{10,1... | collective-permute-start | bytes 2457608 | tf_op jit(solution)/vmap(transpose(jvp()))/dot_general | solution.py:20
  528.2 22.8 %collective-permute-start.2 = (f32[1,64,3200]{2,1,0:T(8,128)S(1)}, f32[1,64,3200]{2,1,0:T(8,128)S(1)}, u32[]{:S(2)}, u32[]{:S(2)}) collective-permute-start(f32[1,64,3200]{2,1,0:T(8,128)S(1)} %get-tuple-element.456), channel_id=5, source_target_pairs={{0,1},{1,2},{2,3},{3,4},{4,5},{5,6},{6,7},{7,8},{8,9},{9,10},{10,1... | collective-permute-start | bytes 2457608 | tf_op jit(solution)/vmap(transpose(jvp()))/dot_general | solution.py:20
  528.3 22.7 %collective-permute-start.3 = (f32[1,64,3200]{2,1,0:T(8,128)S(1)}, f32[1,64,3200]{2,1,0:T(8,128)S(1)}, u32[]{:S(2)}, u32[]{:S(2)}) collective-permute-start(f32[1,64,3200]{2,1,0:T(8,128)S(1)} %get-tuple-element.457), channel_id=4, source_target_pairs={{0,15},{1,0},{2,1},{3,2},{4,3},{5,4},{6,5},{7,6},{8,7},{9,8},{10,9... | collective-permute-start | bytes 2457608 | tf_op jit(solution)/vmap(transpose(jvp()))/dot_general | solution.py:20
  553.3 22.5 %collective-permute-start = (f32[1,64,3200]{2,1,0:T(8,128)S(1)}, f32[1,64,3200]{2,1,0:T(8,128)S(1)}, u32[]{:S(2)}, u32[]{:S(2)}) collective-permute-start(f32[1,64,3200]{2,1,0:T(8,128)S(1)} %broadcast_select_fusion.24), channel_id=3, source_target_pairs={{0,1},{1,2},{2,3},{3,4},{4,5},{5,6},{6,7},{7,8},{8,9},{9,10},{10,1... | collective-permute-start | bytes 2457608 | tf_op jit(solution)/vmap(transpose(jvp()))/dot_general | solution.py:20
  554.3 21.5 %collective-permute-start.1 = (f32[1,64,3200]{2,1,0:T(8,128)}, f32[1,64,3200]{2,1,0:T(8,128)S(1)}, u32[]{:S(2)}, u32[]{:S(2)}) collective-permute-start(f32[1,64,3200]{2,1,0:T(8,128)} %broadcast_select_fusion.25), channel_id=2, source_target_pairs={{0,15},{1,0},{2,1},{3,2},{4,3},{5,4},{6,5},{7,6},{8,7},{9,8},{10,9... | collective-permute-start | bytes 2457608 | tf_op jit(solution)/vmap(transpose(jvp()))/dot_general | solution.py:20
  576.1 19.9 %collective-permute-start.2 = (f32[1,64,3200]{2,1,0:T(8,128)S(1)}, f32[1,64,3200]{2,1,0:T(8,128)S(1)}, u32[]{:S(2)}, u32[]{:S(2)}) collective-permute-start(f32[1,64,3200]{2,1,0:T(8,128)S(1)} %get-tuple-element.456), channel_id=5, source_target_pairs={{0,1},{1,2},{2,3},{3,4},{4,5},{5,6},{6,7},{7,8},{8,9},{9,10},{10,1... | collective-permute-start | bytes 2457608 | tf_op jit(solution)/vmap(transpose(jvp()))/dot_general | solution.py:20
  598.7 21.9 %collective-permute-start = (f32[1,64,3200]{2,1,0:T(8,128)S(1)}, f32[1,64,3200]{2,1,0:T(8,128)S(1)}, u32[]{:S(2)}, u32[]{:S(2)}) collective-permute-start(f32[1,64,3200]{2,1,0:T(8,128)S(1)} %broadcast_select_fusion.24), channel_id=3, source_target_pairs={{0,1},{1,2},{2,3},{3,4},{4,5},{5,6},{6,7},{7,8},{8,9},{9,10},{10,1... | collective-permute-start | bytes 2457608 | tf_op jit(solution)/vmap(transpose(jvp()))/dot_general | solution.py:20
  620.8 22.7 %collective-permute-start.2 = (f32[1,64,3200]{2,1,0:T(8,128)S(1)}, f32[1,64,3200]{2,1,0:T(8,128)S(1)}, u32[]{:S(2)}, u32[]{:S(2)}) collective-permute-start(f32[1,64,3200]{2,1,0:T(8,128)S(1)} %get-tuple-element.456), channel_id=5, source_target_pairs={{0,1},{1,2},{2,3},{3,4},{4,5},{5,6},{6,7},{7,8},{8,9},{9,10},{10,1... | collective-permute-start | bytes 2457608 | tf_op jit(solution)/vmap(transpose(jvp()))/dot_general | solution.py:20
  620.9 22.6 %collective-permute-start.3 = (f32[1,64,3200]{2,1,0:T(8,128)S(1)}, f32[1,64,3200]{2,1,0:T(8,128)S(1)}, u32[]{:S(2)}, u32[]{:S(2)}) collective-permute-start(f32[1,64,3200]{2,1,0:T(8,128)S(1)} %get-tuple-element.457), channel_id=4, source_target_pairs={{0,15},{1,0},{2,1},{3,2},{4,3},{5,4},{6,5},{7,6},{8,7},{9,8},{10,9... | collective-permute-start | bytes 2457608 | tf_op jit(solution)/vmap(transpose(jvp()))/dot_general | solution.py:20
  644.5 813.1 %collective-permute-start.24 = (f32[1,64,3200]{2,1,0:T(8,128)}, f32[1,64,3200]{2,1,0:T(8,128)}, u32[]{:S(2)}, u32[]{:S(2)}) collective-permute-start(f32[1,64,3200]{2,1,0:T(8,128)} %get-tuple-element.37), channel_id=6, source_target_pairs={{0,1},{1,2},{2,3},{3,4},{4,5},{5,6},{6,7},{7,8},{8,9},{9,10},{10,1... | collective-permute-start | bytes 2457608 | tf_op jit(solution)/vmap(transpose(jvp()))/dot_general | solution.py:20
  645.5 31.1 %collective-permute-start.12 = (f32[1,64,3200]{2,1,0:T(8,128)S(1)}, f32[1,64,3200]{2,1,0:T(8,128)S(1)}, u32[]{:S(2)}, u32[]{:S(2)}) collective-permute-start(f32[1,64,3200]{2,1,0:T(8,128)S(1)} %broadcast_select_fusion.30), channel_id=22, source_target_pairs={{0,1},{1,2},{2,3},{3,4},{4,5},{5,6},{6,7},{7,8},{8,9},{9,10},{10,1... | collective-permute-start | bytes 2457608 | tf_op jit(solution)/vmap(transpose(jvp()))/dot_general | solution.py:21
  647.3 29.3 %collective-permute-start.13 = (f32[1,64,3200]{2,1,0:T(8,128)}, f32[1,64,3200]{2,1,0:T(8,128)S(1)}, u32[]{:S(2)}, u32[]{:S(2)}) collective-permute-start(f32[1,64,3200]{2,1,0:T(8,128)} %broadcast_select_fusion.31), channel_id=21, source_target_pairs={{0,15},{1,0},{2,1},{3,2},{4,3},{5,4},{6,5},{7,6},{8,7},{9,8},{10,9... | collective-permute-start | bytes 2457608 | tf_op jit(solution)/vmap(transpose(jvp()))/dot_general | solution.py:21
  676.8 22.4 %collective-permute-start.14 = (f32[1,64,3200]{2,1,0:T(8,128)S(1)}, f32[1,64,3200]{2,1,0:T(8,128)S(1)}, u32[]{:S(2)}, u32[]{:S(2)}) collective-permute-start(f32[1,64,3200]{2,1,0:T(8,128)S(1)} %get-tuple-element.483), channel_id=24, source_target_pairs={{0,1},{1,2},{2,3},{3,4},{4,5},{5,6},{6,7},{7,8},{8,9},{9,10},{10,1... | collective-permute-start | bytes 2457608 | tf_op jit(solution)/vmap(transpose(jvp()))/dot_general | solution.py:21
  676.9 22.3 %collective-permute-start.15 = (f32[1,64,3200]{2,1,0:T(8,128)S(1)}, f32[1,64,3200]{2,1,0:T(8,128)S(1)}, u32[]{:S(2)}, u32[]{:S(2)}) collective-permute-start(f32[1,64,3200]{2,1,0:T(8,128)S(1)} %get-tuple-element.484), channel_id=23, source_target_pairs={{0,15},{1,0},{2,1},{3,2},{4,3},{5,4},{6,5},{7,6},{8,7},{9,8},{10,9... | collective-permute-start | bytes 2457608 | tf_op jit(solution)/vmap(transpose(jvp()))/dot_general | solution.py:21
  701.5 22.5 %collective-permute-start.12 = (f32[1,64,3200]{2,1,0:T(8,128)S(1)}, f32[1,64,3200]{2,1,0:T(8,128)S(1)}, u32[]{:S(2)}, u32[]{:S(2)}) collective-permute-start(f32[1,64,3200]{2,1,0:T(8,128)S(1)} %broadcast_select_fusion.30), channel_id=22, source_target_pairs={{0,1},{1,2},{2,3},{3,4},{4,5},{5,6},{6,7},{7,8},{8,9},{9,10},{10,1... | collective-permute-start | bytes 2457608 | tf_op jit(solution)/vmap(transpose(jvp()))/dot_general | solution.py:21
  702.6 21.4 %collective-permute-start.13 = (f32[1,64,3200]{2,1,0:T(8,128)}, f32[1,64,3200]{2,1,0:T(8,128)S(1)}, u32[]{:S(2)}, u32[]{:S(2)}) collective-permute-start(f32[1,64,3200]{2,1,0:T(8,128)} %broadcast_select_fusion.31), channel_id=21, source_target_pairs={{0,15},{1,0},{2,1},{3,2},{4,3},{5,4},{6,5},{7,6},{8,7},{9,8},{10,9... | collective-permute-start | bytes 2457608 | tf_op jit(solution)/vmap(transpose(jvp()))/dot_general | solution.py:21
  724.2 22.1 %collective-permute-start.14 = (f32[1,64,3200]{2,1,0:T(8,128)S(1)}, f32[1,64,3200]{2,1,0:T(8,128)S(1)}, u32[]{:S(2)}, u32[]{:S(2)}) collective-permute-start(f32[1,64,3200]{2,1,0:T(8,128)S(1)} %get-tuple-element.483), channel_id=24, source_target_pairs={{0,1},{1,2},{2,3},{3,4},{4,5},{5,6},{6,7},{7,8},{8,9},{9,10},{10,1... | collective-permute-start | bytes 2457608 | tf_op jit(solution)/vmap(transpose(jvp()))/dot_general | solution.py:21
  724.3 22.0 %collective-permute-start.15 = (f32[1,64,3200]{2,1,0:T(8,128)S(1)}, f32[1,64,3200]{2,1,0:T(8,128)S(1)}, u32[]{:S(2)}, u32[]{:S(2)}) collective-permute-start(f32[1,64,3200]{2,1,0:T(8,128)S(1)} %get-tuple-element.484), channel_id=23, source_target_pairs={{0,15},{1,0},{2,1},{3,2},{4,3},{5,4},{6,5},{7,6},{8,7},{9,8},{10,9... | collective-permute-start | bytes 2457608 | tf_op jit(solution)/vmap(transpose(jvp()))/dot_general | solution.py:21
  748.5 20.3 %collective-permute-start.12 = (f32[1,64,3200]{2,1,0:T(8,128)S(1)}, f32[1,64,3200]{2,1,0:T(8,128)S(1)}, u32[]{:S(2)}, u32[]{:S(2)}) collective-permute-start(f32[1,64,3200]{2,1,0:T(8,128)S(1)} %broadcast_select_fusion.30), channel_id=22, source_target_pairs={{0,1},{1,2},{2,3},{3,4},{4,5},{5,6},{6,7},{7,8},{8,9},{9,10},{10,1... | collective-permute-start | bytes 2457608 | tf_op jit(solution)/vmap(transpose(jvp()))/dot_general | solution.py:21
  792.2 21.9 %collective-permute-start.12 = (f32[1,64,3200]{2,1,0:T(8,128)S(1)}, f32[1,64,3200]{2,1,0:T(8,128)S(1)}, u32[]{:S(2)}, u32[]{:S(2)}) collective-permute-start(f32[1,64,3200]{2,1,0:T(8,128)S(1)} %broadcast_select_fusion.30), channel_id=22, source_target_pairs={{0,1},{1,2},{2,3},{3,4},{4,5},{5,6},{6,7},{7,8},{8,9},{9,10},{10,1... | collective-permute-start | bytes 2457608 | tf_op jit(solution)/vmap(transpose(jvp()))/dot_general | solution.py:21
  814.3 22.6 %collective-permute-start.14 = (f32[1,64,3200]{2,1,0:T(8,128)S(1)}, f32[1,64,3200]{2,1,0:T(8,128)S(1)}, u32[]{:S(2)}, u32[]{:S(2)}) collective-permute-start(f32[1,64,3200]{2,1,0:T(8,128)S(1)} %get-tuple-element.483), channel_id=24, source_target_pairs={{0,1},{1,2},{2,3},{3,4},{4,5},{5,6},{6,7},{7,8},{8,9},{9,10},{10,1... | collective-permute-start | bytes 2457608 | tf_op jit(solution)/vmap(transpose(jvp()))/dot_general | solution.py:21
  814.4 22.5 %collective-permute-start.15 = (f32[1,64,3200]{2,1,0:T(8,128)S(1)}, f32[1,64,3200]{2,1,0:T(8,128)S(1)}, u32[]{:S(2)}, u32[]{:S(2)}) collective-permute-start(f32[1,64,3200]{2,1,0:T(8,128)S(1)} %get-tuple-element.484), channel_id=23, source_target_pairs={{0,15},{1,0},{2,1},{3,2},{4,3},{5,4},{6,5},{7,6},{8,7},{9,8},{10,9... | collective-permute-start | bytes 2457608 | tf_op jit(solution)/vmap(transpose(jvp()))/dot_general | solution.py:21
  838.0 621.3 %collective-permute-start.27 = (f32[1,64,3200]{2,1,0:T(8,128)}, f32[1,64,3200]{2,1,0:T(8,128)}, u32[]{:S(2)}, u32[]{:S(2)}) collective-permute-start(f32[1,64,3200]{2,1,0:T(8,128)} %get-tuple-element.43), channel_id=25, source_target_pairs={{0,1},{1,2},{2,3},{3,4},{4,5},{5,6},{6,7},{7,8},{8,9},{9,10},{10,1... | collective-permute-start | bytes 2457608 | tf_op jit(solution)/vmap(transpose(jvp()))/dot_general | solution.py:21
  887.5 21.6 %collective-permute-start.8 = (f32[1,64,3200]{2,1,0:T(8,128)}, f32[1,64,3200]{2,1,0:T(8,128)S(1)}, u32[]{:S(2)}, u32[]{:S(2)}) collective-permute-start(f32[1,64,3200]{2,1,0:T(8,128)} %broadcast_select_fusion.28), channel_id=16, source_target_pairs={{0,1},{1,2},{2,3},{3,4},{4,5},{5,6},{6,7},{7,8},{8,9},{9,10},{10,1... | collective-permute-start | bytes 2457608 | tf_op jit(solution)/vmap(transpose(jvp()))/dot_general | solution.py:21
  888.5 20.7 %collective-permute-start.9 = (f32[1,64,3200]{2,1,0:T(8,128)}, f32[1,64,3200]{2,1,0:T(8,128)S(1)}, u32[]{:S(2)}, u32[]{:S(2)}) collective-permute-start(f32[1,64,3200]{2,1,0:T(8,128)} %broadcast_select_fusion.29), channel_id=15, source_target_pairs={{0,15},{1,0},{2,1},{3,2},{4,3},{5,4},{6,5},{7,6},{8,7},{9,8},{10,9... | collective-permute-start | bytes 2457608 | tf_op jit(solution)/vmap(transpose(jvp()))/dot_general | solution.py:21
  909.4 23.3 %collective-permute-start.10 = (f32[1,64,3200]{2,1,0:T(8,128)S(1)}, f32[1,64,3200]{2,1,0:T(8,128)S(1)}, u32[]{:S(2)}, u32[]{:S(2)}) collective-permute-start(f32[1,64,3200]{2,1,0:T(8,128)S(1)} %get-tuple-element.474), channel_id=18, source_target_pairs={{0,1},{1,2},{2,3},{3,4},{4,5},{5,6},{6,7},{7,8},{8,9},{9,10},{10,1... | collective-permute-start | bytes 2457608 | tf_op jit(solution)/vmap(transpose(jvp()))/dot_general | solution.py:21
  909.5 23.2 %collective-permute-start.11 = (f32[1,64,3200]{2,1,0:T(8,128)S(1)}, f32[1,64,3200]{2,1,0:T(8,128)S(1)}, u32[]{:S(2)}, u32[]{:S(2)}) collective-permute-start(f32[1,64,3200]{2,1,0:T(8,128)S(1)} %get-tuple-element.475), channel_id=17, source_target_pairs={{0,15},{1,0},{2,1},{3,2},{4,3},{5,4},{6,5},{7,6},{8,7},{9,8},{10,9... | collective-permute-start | bytes 2457608 | tf_op jit(solution)/vmap(transpose(jvp()))/dot_general | solution.py:21
  935.9 21.5 %collective-permute-start.8 = (f32[1,64,3200]{2,1,0:T(8,128)}, f32[1,64,3200]{2,1,0:T(8,128)S(1)}, u32[]{:S(2)}, u32[]{:S(2)}) collective-permute-start(f32[1,64,3200]{2,1,0:T(8,128)} %broadcast_select_fusion.28), channel_id=16, source_target_pairs={{0,1},{1,2},{2,3},{3,4},{4,5},{5,6},{6,7},{7,8},{8,9},{9,10},{10,1... | collective-permute-start | bytes 2457608 | tf_op jit(solution)/vmap(transpose(jvp()))/dot_general | solution.py:21
  957.7 22.8 %collective-permute-start.10 = (f32[1,64,3200]{2,1,0:T(8,128)S(1)}, f32[1,64,3200]{2,1,0:T(8,128)S(1)}, u32[]{:S(2)}, u32[]{:S(2)}) collective-permute-start(f32[1,64,3200]{2,1,0:T(8,128)S(1)} %get-tuple-element.474), channel_id=18, source_target_pairs={{0,1},{1,2},{2,3},{3,4},{4,5},{5,6},{6,7},{7,8},{8,9},{9,10},{10,1... | collective-permute-start | bytes 2457608 | tf_op jit(solution)/vmap(transpose(jvp()))/dot_general | solution.py:21
  957.8 22.6 %collective-permute-start.11 = (f32[1,64,3200]{2,1,0:T(8,128)S(1)}, f32[1,64,3200]{2,1,0:T(8,128)S(1)}, u32[]{:S(2)}, u32[]{:S(2)}) collective-permute-start(f32[1,64,3200]{2,1,0:T(8,128)S(1)} %get-tuple-element.475), channel_id=17, source_target_pairs={{0,15},{1,0},{2,1},{3,2},{4,3},{5,4},{6,5},{7,6},{8,7},{9,8},{10,9... | collective-permute-start | bytes 2457608 | tf_op jit(solution)/vmap(transpose(jvp()))/dot_general | solution.py:21
  983.7 22.3 %collective-permute-start.8 = (f32[1,64,3200]{2,1,0:T(8,128)}, f32[1,64,3200]{2,1,0:T(8,128)S(1)}, u32[]{:S(2)}, u32[]{:S(2)}) collective-permute-start(f32[1,64,3200]{2,1,0:T(8,128)} %broadcast_select_fusion.28), channel_id=16, source_target_pairs={{0,1},{1,2},{2,3},{3,4},{4,5},{5,6},{6,7},{7,8},{8,9},{9,10},{10,1... | collective-permute-start | bytes 2457608 | tf_op jit(solution)/vmap(transpose(jvp()))/dot_general | solution.py:21
  984.6 21.3 %collective-permute-start.9 = (f32[1,64,3200]{2,1,0:T(8,128)}, f32[1,64,3200]{2,1,0:T(8,128)S(1)}, u32[]{:S(2)}, u32[]{:S(2)}) collective-permute-start(f32[1,64,3200]{2,1,0:T(8,128)} %broadcast_select_fusion.29), channel_id=15, source_target_pairs={{0,15},{1,0},{2,1},{3,2},{4,3},{5,4},{6,5},{7,6},{8,7},{9,8},{10,9... | collective-permute-start | bytes 2457608 | tf_op jit(solution)/vmap(transpose(jvp()))/dot_general | solution.py:21
  1006.2 19.7 %collective-permute-start.10 = (f32[1,64,3200]{2,1,0:T(8,128)S(1)}, f32[1,64,3200]{2,1,0:T(8,128)S(1)}, u32[]{:S(2)}, u32[]{:S(2)}) collective-permute-start(f32[1,64,3200]{2,1,0:T(8,128)S(1)} %get-tuple-element.474), channel_id=18, source_target_pairs={{0,1},{1,2},{2,3},{3,4},{4,5},{5,6},{6,7},{7,8},{8,9},{9,10},{10,1... | collective-permute-start | bytes 2457608 | tf_op jit(solution)/vmap(transpose(jvp()))/dot_general | solution.py:21
  1029.2 19.7 %collective-permute-start.8 = (f32[1,64,3200]{2,1,0:T(8,128)}, f32[1,64,3200]{2,1,0:T(8,128)S(1)}, u32[]{:S(2)}, u32[]{:S(2)}) collective-permute-start(f32[1,64,3200]{2,1,0:T(8,128)} %broadcast_select_fusion.28), channel_id=16, source_target_pairs={{0,1},{1,2},{2,3},{3,4},{4,5},{5,6},{6,7},{7,8},{8,9},{9,10},{10,1... | collective-permute-start | bytes 2457608 | tf_op jit(solution)/vmap(transpose(jvp()))/dot_general | solution.py:21
  1049.1 21.8 %collective-permute-start.10 = (f32[1,64,3200]{2,1,0:T(8,128)S(1)}, f32[1,64,3200]{2,1,0:T(8,128)S(1)}, u32[]{:S(2)}, u32[]{:S(2)}) collective-permute-start(f32[1,64,3200]{2,1,0:T(8,128)S(1)} %get-tuple-element.474), channel_id=18, source_target_pairs={{0,1},{1,2},{2,3},{3,4},{4,5},{5,6},{6,7},{7,8},{8,9},{9,10},{10,1... | collective-permute-start | bytes 2457608 | tf_op jit(solution)/vmap(transpose(jvp()))/dot_general | solution.py:21
  1049.2 21.7 %collective-permute-start.11 = (f32[1,64,3200]{2,1,0:T(8,128)S(1)}, f32[1,64,3200]{2,1,0:T(8,128)S(1)}, u32[]{:S(2)}, u32[]{:S(2)}) collective-permute-start(f32[1,64,3200]{2,1,0:T(8,128)S(1)} %get-tuple-element.475), channel_id=17, source_target_pairs={{0,15},{1,0},{2,1},{3,2},{4,3},{5,4},{6,5},{7,6},{8,7},{9,8},{10,9... | collective-permute-start | bytes 2457608 | tf_op jit(solution)/vmap(transpose(jvp()))/dot_general | solution.py:21
  1073.0 20.3 %collective-permute-start.20 = (f32[1,200,1024]{2,1,0:T(8,128)}, f32[1,200,1024]{2,1,0:T(8,128)S(1)}, u32[]{:S(2)}, u32[]{:S(2)}) collective-permute-start(f32[1,200,1024]{2,1,0:T(8,128)} %broadcast_select_fusion.34), channel_id=35, source_target_pairs={{0,1},{1,2},{2,3},{3,4},{4,5},{5,6},{6,7},{7,8},{8,9},{9,10},{10,1... | collective-permute-start | bytes 2457608 | tf_op jit(solution)/vmap(transpose(jvp()))/dot_general | solution.py:9
  1095.6 21.7 %collective-permute-start.22 = (f32[1,200,1024]{2,1,0:T(8,128)}, f32[1,200,1024]{2,1,0:T(8,128)S(1)}, u32[]{:S(2)}, u32[]{:S(2)}) collective-permute-start(f32[1,200,1024]{2,1,0:T(8,128)} %get-tuple-element.501), channel_id=37, source_target_pairs={{0,1},{1,2},{2,3},{3,4},{4,5},{5,6},{6,7},{7,8},{8,9},{9,10},{10,1... | collective-permute-start | bytes 2457608 | tf_op jit(solution)/vmap(transpose(jvp()))/dot_general | solution.py:9
  1095.6 21.7 %collective-permute-start.23 = (f32[1,200,1024]{2,1,0:T(8,128)S(1)}, f32[1,200,1024]{2,1,0:T(8,128)}, u32[]{:S(2)}, u32[]{:S(2)}) collective-permute-start(f32[1,200,1024]{2,1,0:T(8,128)S(1)} %get-tuple-element.502), channel_id=36, source_target_pairs={{0,15},{1,0},{2,1},{3,2},{4,3},{5,4},{6,5},{7,6},{8,7},{9,8},{10,9... | collective-permute-start | bytes 2457608 | tf_op jit(solution)/vmap(transpose(jvp()))/dot_general | solution.py:9
  1121.7 19.9 %collective-permute-start.20 = (f32[1,200,1024]{2,1,0:T(8,128)}, f32[1,200,1024]{2,1,0:T(8,128)S(1)}, u32[]{:S(2)}, u32[]{:S(2)}) collective-permute-start(f32[1,200,1024]{2,1,0:T(8,128)} %broadcast_select_fusion.34), channel_id=35, source_target_pairs={{0,1},{1,2},{2,3},{3,4},{4,5},{5,6},{6,7},{7,8},{8,9},{9,10},{10,1... | collective-permute-start | bytes 2457608 | tf_op jit(solution)/vmap(transpose(jvp()))/dot_general | solution.py:9
  1143.9 20.6 %collective-permute-start.22 = (f32[1,200,1024]{2,1,0:T(8,128)}, f32[1,200,1024]{2,1,0:T(8,128)S(1)}, u32[]{:S(2)}, u32[]{:S(2)}) collective-permute-start(f32[1,200,1024]{2,1,0:T(8,128)} %get-tuple-element.501), channel_id=37, source_target_pairs={{0,1},{1,2},{2,3},{3,4},{4,5},{5,6},{6,7},{7,8},{8,9},{9,10},{10,1... | collective-permute-start | bytes 2457608 | tf_op jit(solution)/vmap(transpose(jvp()))/dot_general | solution.py:9
  1143.9 20.6 %collective-permute-start.23 = (f32[1,200,1024]{2,1,0:T(8,128)S(1)}, f32[1,200,1024]{2,1,0:T(8,128)}, u32[]{:S(2)}, u32[]{:S(2)}) collective-permute-start(f32[1,200,1024]{2,1,0:T(8,128)S(1)} %get-tuple-element.502), channel_id=36, source_target_pairs={{0,15},{1,0},{2,1},{3,2},{4,3},{5,4},{6,5},{7,6},{8,7},{9,8},{10,9... | collective-permute-start | bytes 2457608 | tf_op jit(solution)/vmap(transpose(jvp()))/dot_general | solution.py:9
  1260.3 20.3 %collective-permute-start.16 = (f32[1,200,1024]{2,1,0:T(8,128)}, f32[1,200,1024]{2,1,0:T(8,128)}, u32[]{:S(2)}, u32[]{:S(2)}) collective-permute-start(f32[1,200,1024]{2,1,0:T(8,128)} %broadcast_select_fusion.32), channel_id=29, source_target_pairs={{0,1},{1,2},{2,3},{3,4},{4,5},{5,6},{6,7},{7,8},{8,9},{9,10},{10,1... | collective-permute-start | bytes 2457608 | tf_op jit(solution)/vmap(transpose(jvp()))/dot_general | solution.py:9
  1307.1 21.4 %collective-permute-start.16 = (f32[1,200,1024]{2,1,0:T(8,128)}, f32[1,200,1024]{2,1,0:T(8,128)}, u32[]{:S(2)}, u32[]{:S(2)}) collective-permute-start(f32[1,200,1024]{2,1,0:T(8,128)} %broadcast_select_fusion.32), channel_id=29, source_target_pairs={{0,1},{1,2},{2,3},{3,4},{4,5},{5,6},{6,7},{7,8},{8,9},{9,10},{10,1... | collective-permute-start | bytes 2457608 | tf_op jit(solution)/vmap(transpose(jvp()))/dot_general | solution.py:9
  1308.1 20.4 %collective-permute-start.17 = (f32[1,200,1024]{2,1,0:T(8,128)}, f32[1,200,1024]{2,1,0:T(8,128)}, u32[]{:S(2)}, u32[]{:S(2)}) collective-permute-start(f32[1,200,1024]{2,1,0:T(8,128)} %broadcast_select_fusion.33), channel_id=28, source_target_pairs={{0,15},{1,0},{2,1},{3,2},{4,3},{5,4},{6,5},{7,6},{8,7},{9,8},{10,9... | collective-permute-start | bytes 2457608 | tf_op jit(solution)/vmap(transpose(jvp()))/dot_general | solution.py:9
  1354.8 22.1 %collective-permute-start.16 = (f32[1,200,1024]{2,1,0:T(8,128)}, f32[1,200,1024]{2,1,0:T(8,128)}, u32[]{:S(2)}, u32[]{:S(2)}) collective-permute-start(f32[1,200,1024]{2,1,0:T(8,128)} %broadcast_select_fusion.32), channel_id=29, source_target_pairs={{0,1},{1,2},{2,3},{3,4},{4,5},{5,6},{6,7},{7,8},{8,9},{9,10},{10,1... | collective-permute-start | bytes 2457608 | tf_op jit(solution)/vmap(transpose(jvp()))/dot_general | solution.py:9
  1355.8 21.1 %collective-permute-start.17 = (f32[1,200,1024]{2,1,0:T(8,128)}, f32[1,200,1024]{2,1,0:T(8,128)}, u32[]{:S(2)}, u32[]{:S(2)}) collective-permute-start(f32[1,200,1024]{2,1,0:T(8,128)} %broadcast_select_fusion.33), channel_id=28, source_target_pairs={{0,15},{1,0},{2,1},{3,2},{4,3},{5,4},{6,5},{7,6},{8,7},{9,8},{10,9... | collective-permute-start | bytes 2457608 | tf_op jit(solution)/vmap(transpose(jvp()))/dot_general | solution.py:9
  1379.5 19.8 %collective-permute-start.18 = (f32[1,200,1024]{2,1,0:T(8,128)}, f32[1,200,1024]{2,1,0:T(8,128)}, u32[]{:S(2)}, u32[]{:S(2)}) collective-permute-start(f32[1,200,1024]{2,1,0:T(8,128)} %get-tuple-element.492), channel_id=31, source_target_pairs={{0,1},{1,2},{2,3},{3,4},{4,5},{5,6},{6,7},{7,8},{8,9},{9,10},{10,1... | collective-permute-start | bytes 2457608 | tf_op jit(solution)/vmap(transpose(jvp()))/dot_general | solution.py:9
  1379.5 19.8 %collective-permute-start.19 = (f32[1,200,1024]{2,1,0:T(8,128)S(1)}, f32[1,200,1024]{2,1,0:T(8,128)}, u32[]{:S(2)}, u32[]{:S(2)}) collective-permute-start(f32[1,200,1024]{2,1,0:T(8,128)S(1)} %get-tuple-element.493), channel_id=30, source_target_pairs={{0,15},{1,0},{2,1},{3,2},{4,3},{5,4},{6,5},{7,6},{8,7},{9,8},{10,9... | collective-permute-start | bytes 2457608 | tf_op jit(solution)/vmap(transpose(jvp()))/dot_general | solution.py:9
  1403.9 20.7 %collective-permute-start.16 = (f32[1,200,1024]{2,1,0:T(8,128)}, f32[1,200,1024]{2,1,0:T(8,128)}, u32[]{:S(2)}, u32[]{:S(2)}) collective-permute-start(f32[1,200,1024]{2,1,0:T(8,128)} %broadcast_select_fusion.32), channel_id=29, source_target_pairs={{0,1},{1,2},{2,3},{3,4},{4,5},{5,6},{6,7},{7,8},{8,9},{9,10},{10,1... | collective-permute-start | bytes 2457608 | tf_op jit(solution)/vmap(transpose(jvp()))/dot_general | solution.py:9
  1449.8 22.0 %collective-permute-start.29 = (f32[1,200,1024]{2,1,0:T(8,128)}, f32[1,200,1024]{2,1,0:T(8,128)}, u32[]{:S(2)}, u32[]{:S(2)}) collective-permute-start(f32[1,200,1024]{2,1,0:T(8,128)} %get-tuple-element.47), channel_id=38, source_target_pairs={{0,1},{1,2},{2,3},{3,4},{4,5},{5,6},{6,7},{7,8},{8,9},{9,10},{10,1... | collective-permute-start | bytes 2457608 | tf_op jit(solution)/vmap(transpose(jvp()))/dot_general | solution.py:9
  1449.8 30.7 %collective-permute-start.28 = (f32[1,200,1024]{2,1,0:T(8,128)}, f32[1,200,1024]{2,1,0:T(8,128)}, u32[]{:S(2)}, u32[]{:S(2)}) collective-permute-start(f32[1,200,1024]{2,1,0:T(8,128)} %get-tuple-element.45), channel_id=32, source_target_pairs={{0,1},{1,2},{2,3},{3,4},{4,5},{5,6},{6,7},{7,8},{8,9},{9,10},{10,1... | collective-permute-start | bytes 2457608 | tf_op jit(solution)/vmap(transpose(jvp()))/dot_general | solution.py:9
  1519.9 215.1 %all-gather.12.cloned.1.call-start = ((), (), s32[]{:S(2)}) async-start(), calls=%async_computation.1 | async-start | bytes 13926400 | tf_op jit(solution)/reshape | solution.py:58
  1525.1 314.5 %all-gather.14.cloned.1.call-start = ((), (), s32[]{:S(2)}) async-start(), calls=%async_computation.2 | async-start | bytes 13926400 | tf_op jit(solution)/reshape | solution.py:58
  (148 other events, 2974.4 us)
Sparse Core Ops, SparseCore 0:
  1520.0 110.3 all-gather.9
  1633.2 101.7 all-gather.11
  1737.8 101.7 all-gather.13
where the time goes:
time: 1890 us; the launch traced here: 1870 us
  waiting for transfers between devices  824 us (44%)
  matrix products  461 us (24%)
  starting transfers between devices  231 us (12%)
  other arithmetic  156 us (8%)
  local copies, waits for them, and re-layouts  105 us (6%)
  loops' own time  49.3 us (3%)
  blocking collectives  30.6 us (2%)
    reshape x3, waiting for transfers between devices, step(): t.reshape(-1, *t.shape[2:])  309 us
    dot_general x34, waiting for transfers between devices, layer(): up = jnp.dot(a, w['w_up'], preferred_element_type=jnp.float32)  186 us
    dot_general x19, matrix products, matmul(): jnp.dot(a, w, preferred_element_type=jnp.float32).astype(jnp.bfloat16)  171 us
    dot_general x34, waiting for transfers between devices, layer(): gate = jnp.dot(a, w['w_gate'], preferred_element_type=jnp.float32)  166 us
    dot_general x34, waiting for transfers between devices, matmul(): jnp.dot(a, w, preferred_element_type=jnp.float32).astype(jnp.bfloat16)  163 us
    dot_general x19, matrix products, layer(): up = jnp.dot(a, w['w_up'], preferred_element_type=jnp.float32)  155 us
    dot_general x19, matrix products, layer(): gate = jnp.dot(a, w['w_gate'], preferred_element_type=jnp.float32)  135 us
    unnamed x63, local copies, waits for them, and re-layouts  88.9 us
  transfers between devices with their start and end apart: 105, of which 60 were waited for; matrix products, arithmetic and copies ran while one was open for 21% of the time, Pallas kernels for 0%

commit v1 on v0

v1 whole, which is shorter than its diff:
```python
import functools

import jax
import jax.numpy as jnp
from jax import lax
from jax.experimental import pallas as pl
from jax.experimental.pallas import tpu as pltpu
from jax.sharding import PartitionSpec as P

MESH = pl.DeviceIdType.MESH
HBM = pltpu.HBM
D, FF, T = 1024, 3200, 2048
bf16, f32 = jnp.bfloat16, jnp.float32
SLOTS = 3


def place():
    me = lax.axis_index("dp")
    return lax.axis_index("rep"), me // 8, lax.rem(me // 2, 4), lax.rem(me, 2)


def device(r, y, z, c):
    return (r, y * 8 + z * 2 + c)


def greet(r, y, z, c):
    bar = pltpu.get_barrier_semaphore()
    peers = [device(r, y, z, 1 - c), device(r, 1 - y, z, c)] + [device(r, y, lax.rem(z + o, 4), c) for o in (1, 2, 3)]
    for p in peers:
        pl.semaphore_signal(bar, 1, device_id=p, device_id_type=MESH)
    pl.semaphore_wait(bar, len(peers))


class Reducer:
    def __init__(self, source, out, sums, rows, cols, total, bufs):
        self.source, self.out, self.sums = source, out, sums
        self.rows, self.cols, self.total = rows, cols, total
        (self.xr, self.xo, self.ys, self.yr, self.s1, self.zs, self.zr, self.go,
         self.xss, self.xrs, self.xls, self.yss, self.yrs, self.zss, self.zrs, self.gos, self.cx, self.cy, self.cz) = bufs
        self.r, self.y, self.z, self.c = place()

    @staticmethod
    def scratch(rows, cols, s=SLOTS):
        V, dma, reg = pltpu.VMEM, pltpu.SemaphoreType.DMA, pltpu.SemaphoreType.REGULAR
        return [
            V((s, 8, rows, cols), bf16), V((s, 8, rows, cols), bf16), V((s, 4, rows, cols), bf16), V((s, 4, rows, cols), bf16),
            V((s, 4, rows, cols), f32), V((s, 3, rows, cols), bf16), V((s, 3, rows, cols), bf16), V((s, rows, cols), bf16),
            dma((s,)), dma((s,)), dma((s,)), dma((s,)), dma((s,)), dma((s, 3)), dma((s, 3)), dma((s,)), reg, reg, reg((3,)),
        ]

    def copies_x(self, q):
        s = lax.rem(q, SLOTS)
        go = pltpu.make_async_remote_copy(
            self.source(q, 1 - self.c), self.xr.at[s], self.xss.at[s], self.xrs.at[s],
            device_id=device(self.r, self.y, self.z, 1 - self.c), device_id_type=MESH)
        own = pltpu.make_async_copy(self.source(q, self.c), self.xo.at[s], self.xls.at[s])
        return go, own

    def copy_y(self, q):
        s = lax.rem(q, SLOTS)
        return pltpu.make_async_remote_copy(
            self.ys.at[s], self.yr.at[s], self.yss.at[s], self.yrs.at[s],
            device_id=device(self.r, 1 - self.y, self.z, self.c), device_id_type=MESH)

    def copy_z(self, q, o):
        s = lax.rem(q, SLOTS)
        return pltpu.make_async_remote_copy(
            self.zs.at[s, o - 1], self.zr.at[s, 3 - o], self.zss.at[s, o - 1], self.zrs.at[s, 3 - o],
            device_id=device(self.r, self.y, lax.rem(self.z + o, 4), self.c), device_id_type=MESH)

    def copy_out(self, q):
        s = lax.rem(q, SLOTS)
        return pltpu.make_async_copy(self.go.at[s], self.out(q), self.gos.at[s])

    def signal(self, sem, dev):
        pl.semaphore_signal(sem, 1, device_id=dev, device_id_type=MESH)

    def stage0(self, q):
        @pl.when(q >= SLOTS)
        def _():
            pl.semaphore_wait(self.cx, 1)

        for copy in self.copies_x(q):
            copy.start()

    def stage1(self, q):
        s = lax.rem(q, SLOTS)
        go, own = self.copies_x(q)
        own.wait()
        go.wait()

        def add(i, _):
            b = (1 - self.y) * 4 + i
            self.ys[s, i] = (self.xo[s, b].astype(f32) + self.xr[s, b].astype(f32)).astype(bf16)
            b = self.y * 4 + i
            self.s1[s, i] = self.xo[s, b].astype(f32) + self.xr[s, b].astype(f32)
            return 0

        lax.fori_loop(0, 4, add, 0)

        @pl.when(q + SLOTS < self.total)
        def _():
            self.signal(self.cx, device(self.r, self.y, self.z, 1 - self.c))

        @pl.when(q >= SLOTS)
        def _():
            pl.semaphore_wait(self.cy, 1)

        self.copy_y(q).start()

    def stage2(self, q):
        s = lax.rem(q, SLOTS)
        self.copy_y(q).wait()
        for o in (1, 2, 3):
            b = lax.rem(self.z + o, 4)
            self.zs[s, o - 1] = (self.s1[s, b] + self.yr[s, b].astype(f32)).astype(bf16)
        self.s1[s, self.z] = self.s1[s, self.z] + self.yr[s, self.z].astype(f32)

        @pl.when(q + SLOTS < self.total)
        def _():
            self.signal(self.cy, device(self.r, 1 - self.y, self.z, self.c))

        for o in (1, 2, 3):

            @pl.when(q >= SLOTS)
            def _():
                pl.semaphore_wait(self.cz.at[o - 1], 1)

            self.copy_z(q, o).start()

    def stage3(self, q):
        s = lax.rem(q, SLOTS)

        @pl.when(q >= SLOTS)
        def _():
            self.copy_out(q - SLOTS).wait()

        for o in (1, 2, 3):
            self.copy_z(q, o).wait()
        total = self.s1[s, self.z] + self.zr[s, 0].astype(f32) + self.zr[s, 1].astype(f32) + self.zr[s, 2].astype(f32)
        total = total.astype(bf16)
        self.go[s] = total
        total = total.astype(f32)
        self.sums[...] += jnp.sum((total * total).reshape(-1, 8, self.cols), 0).reshape(8, -1, 128).sum(1)

        @pl.when(q + SLOTS < self.total)
        def _():
            for o in (1, 2, 3):
                self.signal(self.cz.at[3 - o], device(self.r, self.y, lax.rem(self.z + o, 4), self.c))

        self.copy_out(q).start()

    def tick(self, t, lags=(0, 1, 2, 3)):
        for lag, stage in reversed(list(zip(lags, (self.stage0, self.stage1, self.stage2, self.stage3)))):
            q = t - lag

            @pl.when((q >= 0) & (q < self.total))
            def _():
                stage(q)

    def finish(self):
        for i in range(SLOTS):
            self.copy_out(self.total - SLOTS + i).wait()


GC, GP = 640, 5
DC, DP = 256, 4


def scatter_kernel(dg_ref, dd_ref, g_out, d_out, sums_out, sums, *bufs):
    half = len(bufs) // 2
    r, y, z, c = place()
    greet(r, y, z, c)
    sums[...] = jnp.zeros_like(sums)

    def g_source(q, c):
        m, p = q // GP, lax.rem(q, GP)
        return dg_ref.at[m, :, c, :, pl.ds(pl.multiple_of(p * GC, 128), GC)]

    def g_to(q):
        m, p = q // GP, lax.rem(q, GP)
        return g_out.at[m, :, pl.ds(pl.multiple_of(p * GC, 128), GC)]

    def d_source(q, c):
        m, p = q // DP, lax.rem(q, DP)
        return dd_ref.at[m, :, c, :, pl.ds(pl.multiple_of(p * DC, 128), DC)]

    def d_to(q):
        m, p = q // DP, lax.rem(q, DP)
        return d_out.at[m, :, pl.ds(pl.multiple_of(p * DC, 128), DC)]

    gr = Reducer(g_source, g_to, sums, 64, GC, 4 * GP, bufs[:half])
    dr = Reducer(d_source, d_to, sums, 200, DC, 2 * DP, bufs[half:])
    lax.fori_loop(0, dr.total + 3, lambda t, _: (dr.tick(t), 0)[1], 0)
    dr.finish()
    lax.fori_loop(0, gr.total + 3, lambda t, _: (gr.tick(t), 0)[1], 0)
    gr.finish()
    sums_out[...] = sums[...]


def reduce_scatter(dg, dd):
    return pl.pallas_call(
        scatter_kernel,
        out_shape=(
            jax.ShapeDtypeStruct((4, 64, FF), bf16),
            jax.ShapeDtypeStruct((2, 200, D), bf16),
            jax.ShapeDtypeStruct((8, 128), f32),
        ),
        in_specs=[pl.BlockSpec(memory_space=HBM)] * 2,
        out_specs=(pl.BlockSpec(memory_space=HBM), pl.BlockSpec(memory_space=HBM), pl.BlockSpec(memory_space=pltpu.VMEM)),
        scratch_shapes=[pltpu.VMEM((8, 128), f32)] + Reducer.scratch(64, GC) + Reducer.scratch(200, DC),
        compiler_params=pltpu.CompilerParams(collective_id=0, has_side_effects=True, vmem_limit_bytes=60 * 2**20),
    )(dg.reshape(4, 8, 2, 64, FF), dd.reshape(2, 8, 2, 200, D))


def gather_kernel(sg, su, sd, og, ou, od, zs, zr, ys, yr, ds, dr, ls):
    r, y, z, c = place()
    greet(r, y, z, c)
    chunks = [(s, o, layer) for layer in range(2) for s, o in ((sg, og), (su, ou), (sd, od))]
    n = len(chunks)

    def block(y, z, c):
        return y * 8 + z * 2 + c

    def zat(o):
        return lax.rem(z + o, 4)

    partner, across = device(r, y, z, 1 - c), device(r, 1 - y, z, c)
    mine = block(y, z, c)
    sent = []

    def send(src, k, b, ssem, rsem, dev):
        _, o, layer = chunks[k]
        copy = pltpu.make_async_remote_copy(src, o.at[layer, b], ssem, rsem, device_id=dev, device_id_type=MESH)
        copy.start()
        sent.append(copy)

    def arrived(k, b, ssem, rsem, dev):
        _, o, layer = chunks[k]
        ref = o.at[layer, b]
        pltpu.make_async_remote_copy(ref, ref, ssem, rsem, device_id=dev, device_id_type=MESH).wait_recv()
        return ref

    local = []
    for k, (s, o, layer) in enumerate(chunks):
        for d in (1, 2, 3):
            send(s.at[layer], k, mine, zs.at[k, d - 1], zr.at[k, 3 - d], device(r, y, zat(d), c))
        send(s.at[layer], k, mine, ys.at[k, 0], yr.at[k, 0], across)
        send(s.at[layer], k, mine, ds.at[k, 0], dr.at[k, 0], partner)
        copy = pltpu.make_async_copy(s.at[layer], o.at[layer, mine], ls.at[k])
        copy.start()
        local.append(copy)
    for k in range(n + 1):
        if k < n:
            for d in (1, 2, 3):
                b = block(y, zat(d), c)
                ref = arrived(k, b, zs.at[k, d - 1], zr.at[k, d - 1], across)
                send(ref, k, b, ys.at[k, d], yr.at[k, d], across)
                send(ref, k, b, ds.at[k, d], dr.at[k, d], partner)
        if k >= 1:
            for d in range(4):
                b = block(1 - y, zat(d), c)
                ref = arrived(k - 1, b, ys.at[k - 1, d], yr.at[k - 1, d], across)
                send(ref, k - 1, b, ds.at[k - 1, 4 + d], dr.at[k - 1, 4 + d], partner)
    for k in range(n):
        for e in range(8):
            b = block(y if e < 4 else 1 - y, zat(e % 4), 1 - c)
            arrived(k, b, ds.at[k, e], dr.at[k, e], partner)
    for copy in sent:
        copy.wait_send()
    for copy in local:
        copy.wait()


def all_gather(sg, su, sd):
    dma = pltpu.SemaphoreType.DMA
    out = pl.pallas_call(
        gather_kernel,
        out_shape=(
            jax.ShapeDtypeStruct((2, 16, 64, FF), bf16),
            jax.ShapeDtypeStruct((2, 16, 64, FF), bf16),
            jax.ShapeDtypeStruct((2, 16, 200, D), bf16),
        ),
        in_specs=[pl.BlockSpec(memory_space=pltpu.VMEM)] * 3,
        out_specs=[pl.BlockSpec(memory_space=HBM)] * 3,
        scratch_shapes=[dma((6, 3)), dma((6, 3)), dma((6, 4)), dma((6, 4)), dma((6, 8)), dma((6, 8)), dma((6,))],
        compiler_params=pltpu.CompilerParams(collective_id=1, has_side_effects=True),
    )(sg, su, sd)
    return out[0].reshape(2, D, FF), out[1].reshape(2, D, FF), out[2].reshape(2, FF, D)


def dot(a, b, ca, cb):
    return lax.dot_general(a, b, (((ca,), (cb,)), ((), ())), preferred_element_type=f32)


def normed(h):
    wide = h.astype(f32)
    return (wide * lax.rsqrt(jnp.mean(wide**2, -1, keepdims=True) + 1e-6)).astype(bf16)


def normed_back(h, da):
    wide, da = h.astype(f32), da.astype(f32)
    scale = lax.rsqrt(jnp.mean(wide**2, -1, keepdims=True) + 1e-6)
    inner = jnp.mean(da * wide, -1, keepdims=True)
    return scale * da - wide * (scale**3 * inner)


def layer_back(a, gate, up, mid, wd, dh):
    dmid = dot(dh, wd, 1, 1).astype(bf16).astype(f32)
    sig = jax.nn.sigmoid(gate)
    silu = gate * sig
    dgate = (dmid * up * (sig + silu * (1 - sig))).astype(bf16)
    dup = (dmid * silu).astype(bf16)
    return dot(a, dgate, 0, 0).astype(bf16), dot(a, dup, 0, 0).astype(bf16), dot(mid, dh, 0, 0).astype(bf16), dgate, dup


def local_terms(x, dy, wg, wu, wd):
    h, kept = x, []
    for i in range(2):
        a = normed(h)
        gate, up = dot(a, wg[i], 1, 0), dot(a, wu[i], 1, 0)
        mid = (jax.nn.silu(gate) * up).astype(bf16)
        kept.append((h, a, gate, up, mid))
        if i == 0:
            h = h + dot(mid, wd[i], 1, 0).astype(bf16)
    h1, a1, gate1, up1, mid1 = kept[1]
    dwg1, dwu1, dwd1, dgate, dup = layer_back(a1, gate1, up1, mid1, wd[1], dy)
    da = dot(dgate, wg[1], 1, 1) + dot(dup, wu[1], 1, 1)
    dh = dy + normed_back(h1, da).astype(bf16)
    _, a0, gate0, up0, mid0 = kept[0]
    dwg0, dwu0, dwd0, _, _ = layer_back(a0, gate0, up0, mid0, wd[0], dh)
    return jnp.stack([dwg1, dwu1, dwg0, dwu0]), jnp.stack([dwd1, dwd0])


def adamw(w, m, v, g):
    m = 0.9 * m + 0.1 * g
    v = 0.95 * v + 0.05 * g * g
    step = m * lax.rsqrt(v + 1e-8) + 0.1 * w
    return (w - 0.02 * step).astype(bf16), m, v


def solution(mesh):
    def step(x, dy, wg, wu, wd, mg, mu, md, vg, vu, vd):
        dg, dd = local_terms(x[0], dy[0], wg, wu, wd)
        gg, gd, sums = reduce_scatter(dg, dd)
        squares = lax.psum(jnp.sum(sums), "dp")
        factor = jnp.minimum(1.0, 0.5 * lax.rsqrt(squares / (6 * D * FF) + 1e-30))
        me = lax.axis_index("dp")
        new = []
        for w, m, v, g in ((wg, mg, vg, gg[2::-2]), (wu, mu, vu, gg[3::-2]), (wd, md, vd, gd[::-1])):
            rows = m.shape[1]
            mine = lax.dynamic_slice_in_dim(w, me * rows, rows, 1)
            new.append(adamw(mine.astype(f32), m, v, g.astype(f32) * factor))
        weights = all_gather(*(n[0] for n in new))
        return (*weights, *(n[1] for n in new), *(n[2] for n in new))

    seq, rep, own = P(("rep", "dp")), P("rep"), P("rep", "dp")
    return jax.shard_map(
        step,
        mesh=mesh,
        in_specs=(seq, seq, P(), P(), P(), *[P(None, "dp")] * 6),
        out_specs=(rep,) * 3 + (own,) * 6,
        check_vma=False,
    )
```

time: 1890 us -> 1060 us (0.56)
  the two profiles are of different devices: /device:TPU:0 before, /device:TPU:11 now
where the time goes in v1:
time: 1060 us; the launch traced here: 1050 us
  Pallas kernels  560 us (53%)
  matrix products  371 us (35%)
  other arithmetic  47.4 us (4%)
  local copies, waits for them, and re-layouts  40.5 us (4%)
  blocking collectives  30.6 us (3%)
    dot_general x15, matrix products, dot(): lax.dot_general(a, b, (((ca,), (cb,)), ((), ())), preferred_element_type=...  371 us
    pallas_call x1, Pallas kernels, reduce_scatter(): pl.pallas_call(scatter_kernel, out_shape=(jax.ShapeDtypeStruct((4, 64, FF...  282 us
    pallas_call x1, Pallas kernels, all_gather(): pl.pallas_call(gather_kernel, out_shape=(jax.ShapeDtypeStruct((2, 16, 64,...  278 us
    unnamed x39, local copies, waits for them, and re-layouts  40.3 us
    psum x1, blocking collectives, step(): squares = lax.psum(jnp.sum(sums), 'dp')  30.6 us
    another operation x2, other arithmetic, local_terms(): return (jnp.stack([dwg1, dwu1, dwg0, dwu0]), jnp.stack([dwd1, dwd0]))  24.2 us

profile of v1, /device:TPU:11, one launch (start us, length us, event | category | flops | bytes accessed | tf_op | source)
XLA Modules:
  0.0 1051.1 jit_solution(17801037234549170887)
XLA Ops:
  0.6 6.5 copy.20
  7.2 3.1 fusion.13
  10.2 0.0 copy-start.9
  10.2 21.9 %fusion.41 = f32[2048,3200]{1,0:T(8,128)} fusion(bf16[2,1024,3200]{2,1,0:T(8,128)(2,1)} %param.13, bf16[1,2048,1024]{2,1,0:T(8,128)(2,1)} %param.11, f32[2048]{0:T(1024)S(1)} %add_rsqrt_fusion.1), kind=kOutput, calls=%fused_computation.57 | convolution fusion | flops 13428064256 | bytes 36970496 | tf_op jit(solution)/shard_map/dot_general | solution.py:293
  32.1 0.0 copy-done.9
  32.1 32.1 %multiply_convert_fusion.1 = (bf16[2048,3200]{1,0:T(8,128)(2,1)}, f32[2048,3200]{1,0:T(8,128)}) fusion(f32[2048,3200]{1,0:T(8,128)} %fusion.41, bf16[2,1024,3200]{2,1,0:T(8,128)(2,1)} %param.14, bf16[1,2048,1024]{2,1,0:T(8,128)(2,1)} %param.11, f32[2048]{0:T(1024)S(1)} %add_rsqrt_fusion.1), kind=kOutput, calls=%fused_computation.13 | convolution fusion | flops 13467385856 | bytes 76292096 | tf_op jit(solution)/shard_map/dot_general | solution.py:293
  64.2 22.1 %fusion.15 = (f32[2048]{0:T(1024)S(1)}, bf16[2048,1024]{0,1:T(8,128)(2,1)}) fusion(bf16[2048,3200]{1,0:T(8,128)(2,1)} %get-tuple-element.32, bf16[2,3200,1024]{2,1,0:T(8,128)(2,1)} %param.15, bf16[1,2048,1024]{1,2,0:T(8,128)(2,1)} %copy.20), kind=kOutput, calls=%fused_computation.31 | convolution fusion | flops 13432256512 | bytes 28057600 | tf_op jit(solution)/shard_map/dot_general | solution.py:293
  86.3 0.0 copy-start.7
  86.3 0.6 copy-done.7
  86.9 0.0 copy-start.2
  86.9 23.4 %fusion.29 = f32[2048,3200]{1,0:T(8,128)} fusion(bf16[2,1024,3200]{2,1,0:T(8,128)(2,1)} %param.13, bf16[2048,1024]{0,1:T(8,128)(2,1)} %get-tuple-element.35, f32[2048]{0:T(1024)S(1)} %add_rsqrt_fusion), kind=kOutput, calls=%fused_computation.45 | convolution fusion | flops 13428064256 | bytes 36970496 | tf_op jit(solution)/shard_map/dot_general | solution.py:293
  110.3 0.0 copy-done.2
  110.3 19.5 %convolution_convert_fusion.1 = bf16[2048,3200]{1,0:T(8,128)(2,1)} fusion(bf16[2,3200,1024]{2,1,0:T(8,128)(2,1)} %param.15, bf16[1,2048,1024]{2,1,0:T(8,128)(2,1)S(1)} %copy-done.2), kind=kOutput, calls=%fused_computation.18 | convolution fusion | flops 13428326400 | bytes 23855104 | tf_op jit(solution)/shard_map/dot_general | solution.py:293
  129.9 37.9 %fusion.1 = (bf16[2048,3200]{1,0:T(8,128)(2,1)}, f32[2048,3200]{1,0:T(8,128)}) fusion(bf16[2048,3200]{1,0:T(8,128)(2,1)} %convolution_convert_fusion.1, f32[2048,3200]{1,0:T(8,128)} %fusion.29, bf16[2,1024,3200]{2,1,0:T(8,128)(2,1)} %param.14, bf16[2048,1024]{0,1:T(8,128)(2,1)} %get-tuple-element.35, f32[2048]{0:T(1024)S(1)} %add_rsqrt_fusion), kind=kOutput, calls=%fused_computation.5 | convolution fusion | flops 13500153856 | bytes 89399296 | tf_op jit(solution)/shard_map/dot_general | solution.py:293
  167.8 25.7 %fusion.26 = bf16[3200,1024]{1,0:T(8,128)(2,1)} fusion(f32[2048,3200]{1,0:T(8,128)} %get-tuple-element.37, bf16[1,2048,1024]{2,1,0:T(8,128)(2,1)} %param.12, f32[2048,3200]{1,0:T(8,128)} %fusion.29), kind=kOutput, calls=%fused_computation.39 | convolution fusion | flops 13464371200 | bytes 63176704 | tf_op jit(solution)/shard_map/dot_general | solution.py:293
  193.5 20.3 %fusion.27 = f32[2048,1024]{0,1:T(8,128)} fusion(bf16[2048,3200]{1,0:T(8,128)(2,1)} %get-tuple-element.36, bf16[2,1024,3200]{2,1,0:T(8,128)(2,1)} %param.13), kind=kOutput, calls=%fused_computation.43 | convolution fusion | flops 13421772800 | bytes 28049408 | tf_op jit(solution)/shard_map/dot_general | solution.py:293
  213.8 0.0 copy-start.8
  213.8 27.7 %fusion.17 = (f32[2048]{0:T(1024)S(1)}, f32[2048,1024]{0,1:T(8,128)}) fusion(bf16[2048,1024]{0,1:T(8,128)(2,1)} %get-tuple-element.35, f32[2048,1024]{0,1:T(8,128)} %fusion.27, bf16[2,1024,3200]{2,1,0:T(8,128)(2,1)} %param.14, bf16[2048,3200]{1,0:T(8,128)(2,1)} %convolution_convert_fusion.1, f32[2048,3200]{1,0:T(8,128)} %fusion.29), kind=kOutput, calls=%fused_computation.33 | convolution fusion | flops 13476034560 | bytes 66854912 | tf_op jit(solution)/shard_map/dot_general | solution.py:293
  241.4 0.0 copy-done.8
  241.5 6.5 copy.21
  247.9 0.0 slice-start.4
  247.9 8.9 fusion.56
  256.9 0.0 slice-start.5
  256.9 19.7 %convolution_convert_fusion.2 = bf16[3200,1024]{1,0:T(8,128)(2,1)S(1)} fusion(bf16[2048,3200]{1,0:T(8,128)(2,1)} %get-tuple-element.32, bf16[2048,1024]{0,1:T(8,128)(2,1)} %fusion.56), kind=kOutput, calls=%fused_computation.40 | convolution fusion | flops 13425049600 | bytes 23855104 | tf_op jit(solution)/shard_map/dot_general | solution.py:293
  276.5 0.0 slice-done.4
  276.6 0.0 slice-done.5
  276.6 0.0 copy-start.3
  276.6 5.6 pad_maximum_fusion.1.dd_ref
  282.1 0.0 copy-done.3
  282.1 20.2 %convolution_convert_fusion.4 = bf16[1024,3200]{1,0:T(8,128)(2,1)} fusion(bf16[2048,3200]{1,0:T(8,128)(2,1)} %get-tuple-element.36, bf16[2048,1024]{0,1:T(8,128)(2,1)S(1)} %copy-done.3, f32[2048]{0:T(1024)S(1)} %add_rsqrt_fusion), kind=kOutput, calls=%fused_computation.42 | convolution fusion | flops 13431341056 | bytes 23863296 | tf_op jit(solution)/shard_map/dot_general | solution.py:293
  302.4 0.0 copy-start.10
  302.4 21.2 %convolution_convert_fusion = bf16[2048,3200]{1,0:T(8,128)(2,1)} fusion(bf16[2048,1024]{0,1:T(8,128)(2,1)} %fusion.56, bf16[2,3200,1024]{2,1,0:T(8,128)(2,1)} %param.15), kind=kOutput, calls=%fused_computation.17 | convolution fusion | flops 13428326400 | bytes 23855104 | tf_op jit(solution)/shard_map/dot_general | solution.py:293
  323.5 0.0 copy-done
  323.5 0.0 copy-done.10
  323.5 29.6 %fusion.20 = bf16[1024,3200]{1,0:T(8,128)(2,1)} fusion(f32[2048,3200]{1,0:T(8,128)} %get-tuple-element.33, bf16[2048,3200]{1,0:T(8,128)(2,1)} %convolution_convert_fusion, f32[2048,3200]{1,0:T(8,128)} %fusion.41, bf16[1,2048,1024]{1,2,0:T(8,128)(2,1)S(1)} %copy-done, f32[2048]{0:T(1024)S(1)} %copy-done.10), kind=kOutput, calls=%fused_computation.37 | convolution fusion | flops 13503430656 | bytes 76292096 | tf_op jit(solution)/shard_map/dot_general | solution.py:293
  353.1 24.3 %fusion.23 = bf16[1024,3200]{1,0:T(8,128)(2,1)} fusion(bf16[2048,3200]{1,0:T(8,128)(2,1)} %convolution_convert_fusion, bf16[1,2048,1024]{1,2,0:T(8,128)(2,1)S(1)} %copy-done, f32[2048]{0:T(1024)S(1)} %copy-done.10, f32[2048,3200]{1,0:T(8,128)} %fusion.41), kind=kOutput, calls=%fused_computation.38 | convolution fusion | flops 13477216256 | bytes 50077696 | tf_op jit(solution)/shard_map/dot_general | solution.py:293
  377.4 25.2 %convolution_convert_fusion.3 = bf16[1024,3200]{1,0:T(8,128)(2,1)} fusion(bf16[2048,1024]{0,1:T(8,128)(2,1)} %get-tuple-element.35, f32[2048]{0:T(1024)S(1)} %add_rsqrt_fusion, bf16[2048,3200]{1,0:T(8,128)(2,1)} %convolution_convert_fusion.1, f32[2048,3200]{1,0:T(8,128)} %fusion.29), kind=kOutput, calls=%fused_computation.41 | convolution fusion | flops 13477216256 | bytes 50077696 | tf_op jit(solution)/shard_map/dot_general | solution.py:293
  402.6 18.6 %pad_maximum_fusion.dg_ref = bf16[4,8,2,64,3200]{4,3,2,1,0:T(8,128)(2,1)} fusion(bf16[1,8,2,64,3200]{4,3,2,1,0:T(8,128)(2,1)} %bitcast.78, bf16[1,8,2,64,3200]{4,3,2,1,0:T(8,128)(2,1)} %bitcast.77, bf16[1,8,2,64,3200]{4,3,2,1,0:T(8,128)(2,1)} %bitcast.79, bf16[1,8,2,64,3200]{4,3,2,1,0:T(8,128)(2,1)} %bitcast.76), kind=kLoop, calls=%fused_computation.10 | loop fusion | flops 39321600 | bytes 52428800 | tf_op jit(solution)/shard_map/stack | solution.py:332
  421.2 0.0 copy-start.4
  421.2 0.0 copy-start.5
  421.2 282.3 %shard_map.178 = (bf16[4,64,3200]{2,1,0:T(8,128)(2,1)}, bf16[2,200,1024]{2,1,0:T(8,128)(2,1)}, f32[8,128]{1,0:T(8,128)}) custom-call(bf16[4,8,2,64,3200]{4,3,2,1,0:T(8,128)(2,1)} %pad_maximum_fusion.dg_ref, bf16[2,8,2,200,1024]{4,3,2,1,0:T(8,128)(2,1)} %pad_maximum_fusion.1.dd_ref), custom_call_target="tpu_custom_call" | custom-call | tf_op jit(solution)/shard_map/pallas_call | solution.py:202
  703.6 1.3 reduce_sum.43
  704.8 30.6 %psum.7 = f32[]{:T(128)} all-reduce(f32[]{:T(128)} %reduce_sum.43), channel_id=1, replica_groups=mesh['rep'=2,'dp'=16] {'dp'}, use_global_device_ids=true, to_apply=%region_4.5 | all-reduce | flops 1 | bytes 8 | tf_op jit(solution)/shard_map/psum | solution.py:346
  736.2 0.0 copy-done.4
  736.2 0.0 copy-done.5
  736.2 0.0 copy-start.6
  736.2 4.0 fusion.77
  740.2 0.0 copy-done.6
  740.2 0.1 fusion.93
  740.4 6.0 fusion.71
  746.3 277.5 %shard_map.179 = (bf16[2,16,64,3200]{3,2,1,0:T(8,128)(2,1)}, bf16[2,16,64,3200]{3,2,1,0:T(8,128)(2,1)}, bf16[2,16,200,1024]{3,2,1,0:T(8,128)(2,1)}) custom-call(bf16[2,64,3200]{2,1,0:T(8,128)(2,1)} %get-tuple-element.27.sg, bf16[2,64,3200]{2,1,0:T(8,128)(2,1)} %get-tuple-element.40.su, bf16[2,200,1024]{2,1,0:T(8,128)(2,1)} %get-tuple-element.21.sd), custom_call_target="tpu_custom_call" | custom-call | tf_op jit(solution)/shard_map/pallas_call | solution.py:277
  1023.9 0.0 copy-start.1
  1023.9 0.0 slice-start
  1023.9 0.0 slice-start.1
  1023.9 12.7 %copy.25 = bf16[2,1024,3200]{2,1,0:T(8,128)(2,1)} copy(bf16[2,1024,3200]{2,1,0:T(8,128)(2,1)} %bitcast.75) | data formatting | bytes 26214400
  1036.6 0.0 copy-done.1
  1036.6 0.0 slice-start.2
  1036.6 0.0 slice-start.3
  1036.6 6.6 copy.26
  1043.2 0.0 slice-done
  1043.2 1.2 slice-done.1
  1044.4 1.3 slice-done.2
  1045.6 0.0 slice-done.3
  1045.7 4.9 copy.27
  (6 shorter events, 0.0 us)
Async XLA Ops:
  10.2 21.9 %copy-start.9 = (f32[2048]{0:T(1024)}, f32[2048]{0:T(1024)S(1)}, u32[]{:S(2)}) copy-start(f32[2048]{0:T(1024)S(1)} %add_rsqrt_fusion.1) | copy-start | bytes 24580
  86.3 0.6 copy-start.7
  86.9 23.4 %copy-start.2 = (bf16[1,2048,1024]{2,1,0:T(8,128)(2,1)S(1)}, bf16[1,2048,1024]{2,1,0:T(8,128)(2,1)}, u32[]{:S(2)}) copy-start(bf16[1,2048,1024]{2,1,0:T(8,128)(2,1)} %param.12) | copy-start | bytes 12582916
  213.8 27.7 %copy-start.8 = (f32[2048]{0:T(1024)S(1)}, f32[2048]{0:T(1024)}, u32[]{:S(2)}) copy-start(f32[2048]{0:T(1024)} %copy-done.7) | copy-start | bytes 24580
  247.9 28.6 %slice-start.4 = ((s8[6553600]{0:T(1024)(128)(4,1)}), s8[4194304]{0:T(1024)(128)(4,1)S(1)}, s32[]{:S(2)}) async-start(s8[6553600]{0:T(1024)(128)(4,1)} %bitcast.80), calls=%async_computation.4 | async-start | bytes 8388608
  256.9 19.7 %slice-start.5 = ((s8[6553600]{0:T(1024)(128)(4,1)}), s8[2359296]{0:T(1024)(128)(4,1)S(1)}, s32[]{:S(2)}) async-start(s8[6553600]{0:T(1024)(128)(4,1)} %bitcast.80), calls=%async_computation.5 | async-start | bytes 4718592
  276.6 5.6 copy-start.3
  302.4 21.2 %copy-start = (bf16[1,2048,1024]{1,2,0:T(8,128)(2,1)S(1)}, bf16[1,2048,1024]{1,2,0:T(8,128)(2,1)}, u32[]{:S(2)}) copy-start(bf16[1,2048,1024]{1,2,0:T(8,128)(2,1)} %copy.20) | copy-start | bytes 12582916
  302.4 21.2 %copy-start.10 = (f32[2048]{0:T(1024)S(1)}, f32[2048]{0:T(1024)}, u32[]{:S(2)}) copy-start(f32[2048]{0:T(1024)} %copy-done.9) | copy-start | bytes 24580
  421.2 315.0 %copy-start.4 = (f32[2,200,1024]{2,1,0:T(8,128)S(1)}, f32[2,200,1024]{2,1,0:T(8,128)}, u32[]{:S(2)}) copy-start(f32[2,200,1024]{2,1,0:T(8,128)} %param.21) | copy-start | bytes 4915204
  421.2 315.0 %copy-start.5 = (f32[2,200,1024]{2,1,0:T(8,128)S(1)}, f32[2,200,1024]{2,1,0:T(8,128)}, u32[]{:S(2)}) copy-start(f32[2,200,1024]{2,1,0:T(8,128)} %param.18) | copy-start | bytes 4915204
  736.2 4.0 copy-start.6
  1023.9 12.7 %copy-start.1 = (bf16[2,16,64,3200]{3,2,1,0:T(8,128)(2,1)S(1)}, bf16[2,16,64,3200]{3,2,1,0:T(8,128)(2,1)}, u32[]{:S(2)}) copy-start(bf16[2,16,64,3200]{3,2,1,0:T(8,128)(2,1)} %get-tuple-element.19) | copy-start | bytes 39321604
  1023.9 19.4 %slice-start = ((s8[13107200]{0:T(1024)(128)(4,1)}), s8[4194304]{0:T(1024)(128)(4,1)S(1)}, s32[]{:S(2)}) async-start(s8[13107200]{0:T(1024)(128)(4,1)} %bitcast.71), calls=%async_computation | async-start | bytes 8388608
  1023.9 20.5 %slice-start.1 = ((s8[13107200]{0:T(1024)(128)(4,1)}), s8[4194304]{0:T(1024)(128)(4,1)S(1)}, s32[]{:S(2)}) async-start(s8[13107200]{0:T(1024)(128)(4,1)} %bitcast.71), calls=%async_computation.1 | async-start | bytes 8388608
  1036.6 9.1 slice-start.2
  1036.6 9.1 slice-start.3

commit v2 on v1

v2 whole, which is shorter than its diff:
```python
import functools

import jax
import jax.numpy as jnp
from jax import lax
from jax.experimental import pallas as pl
from jax.experimental.pallas import tpu as pltpu
from jax.sharding import PartitionSpec as P

MESH = pl.DeviceIdType.MESH
HBM = pltpu.HBM
D, FF, T = 1024, 3200, 2048
bf16, f32 = jnp.bfloat16, jnp.float32


def place():
    me = lax.axis_index("dp")
    return lax.axis_index("rep"), me // 8, lax.rem(me // 2, 4), lax.rem(me, 2)


def device(r, y, z, c):
    return (r, y * 8 + z * 2 + c)


def greet(r, y, z, c):
    bar = pltpu.get_barrier_semaphore()
    peers = [device(r, y, z, 1 - c), device(r, 1 - y, z, c)] + [device(r, y, lax.rem(z + o, 4), c) for o in (1, 2, 3)]
    for p in peers:
        pl.semaphore_signal(bar, 1, device_id=p, device_id_type=MESH)
    pl.semaphore_wait(bar, len(peers))


def dot(a, b, ca, cb):
    return lax.dot_general(a, b, (((ca,), (cb,)), ((), ())), preferred_element_type=f32)


class Reducer:
    LAGS = (0, 1, 3, 5)

    def __init__(self, source, own, out, sums, slots, total, bufs):
        self.source, self.own, self.out, self.sums, self.total = source, own, out, sums, total
        self.nx, self.ny, self.nz = slots
        (self.xr, self.ys, self.yr, self.s1, self.acc, self.zs, self.zr, self.go,
         self.xss, self.xrs, self.yss, self.yrs, self.zss, self.zrs, self.gos, self.cx, self.cy, self.cz) = bufs
        self.r, self.y, self.z, self.c = place()

    @staticmethod
    def scratch(shape, parts, slots):
        nx, ny, nz = slots
        V, dma, reg = pltpu.VMEM, pltpu.SemaphoreType.DMA, pltpu.SemaphoreType.REGULAR
        return [
            V((nx, 8, *shape), bf16), V((ny, 4, *shape), bf16), V((ny, 4, *shape), bf16), V((ny, 4, *shape), f32),
            V((nz, *shape), f32), V((nz, 3, *shape), bf16), V((nz, 3, *shape), bf16), V((nz, *shape), bf16),
            dma((nx, parts)), dma((nx, parts)), dma((ny,)), dma((ny,)), dma((nz, 3)), dma((nz, 3)), dma((nz,)), reg, reg, reg((3,)),
        ]

    def copies_x(self, q):
        s = lax.rem(q, self.nx)
        return [
            pltpu.make_async_remote_copy(
                src, self.xr.at[s] if b is None else self.xr.at[s, b], self.xss.at[s, b or 0], self.xrs.at[s, b or 0],
                device_id=device(self.r, self.y, self.z, 1 - self.c), device_id_type=MESH)
            for src, b in self.source(q, 1 - self.c)
        ]

    def copy_y(self, q):
        s = lax.rem(q, self.ny)
        return pltpu.make_async_remote_copy(
            self.ys.at[s], self.yr.at[s], self.yss.at[s], self.yrs.at[s],
            device_id=device(self.r, 1 - self.y, self.z, self.c), device_id_type=MESH)

    def copy_z(self, q, o):
        s = lax.rem(q, self.nz)
        return pltpu.make_async_remote_copy(
            self.zs.at[s, o - 1], self.zr.at[s, 3 - o], self.zss.at[s, o - 1], self.zrs.at[s, 3 - o],
            device_id=device(self.r, self.y, lax.rem(self.z + o, 4), self.c), device_id_type=MESH)

    def copy_out(self, q):
        s = lax.rem(q, self.nz)
        return pltpu.make_async_copy(self.go.at[s], self.out(q), self.gos.at[s])

    def signal(self, sem, dev):
        pl.semaphore_signal(sem, 1, device_id=dev, device_id_type=MESH)

    def stage0(self, q):
        @pl.when(q >= self.nx)
        def _():
            pl.semaphore_wait(self.cx, 1)

        for copy in self.copies_x(q):
            copy.start()
        self.own.start(q)

    def stage1(self, q):
        x, s = lax.rem(q, self.nx), lax.rem(q, self.ny)
        self.own.wait(q)
        for copy in self.copies_x(q):
            copy.wait()

        def add(i, _):
            b = (1 - self.y) * 4 + i
            self.ys[s, i] = (self.own.read(q, b).astype(f32) + self.xr[x, b].astype(f32)).astype(bf16)
            b = self.y * 4 + i
            self.s1[s, i] = self.own.read(q, b).astype(f32) + self.xr[x, b].astype(f32)
            return 0

        lax.fori_loop(0, 4, add, 0)

        @pl.when(q + self.nx < self.total)
        def _():
            self.signal(self.cx, device(self.r, self.y, self.z, 1 - self.c))

        @pl.when(q >= self.ny)
        def _():
            pl.semaphore_wait(self.cy, 1)

        self.copy_y(q).start()

    def stage2(self, q):
        s, t = lax.rem(q, self.ny), lax.rem(q, self.nz)
        self.copy_y(q).wait()
        for o in (1, 2, 3):
            b = lax.rem(self.z + o, 4)
            self.zs[t, o - 1] = (self.s1[s, b] + self.yr[s, b].astype(f32)).astype(bf16)
        self.acc[t] = self.s1[s, self.z] + self.yr[s, self.z].astype(f32)

        @pl.when(q + self.ny < self.total)
        def _():
            self.signal(self.cy, device(self.r, 1 - self.y, self.z, self.c))

        for o in (1, 2, 3):

            @pl.when(q >= self.nz)
            def _():
                pl.semaphore_wait(self.cz.at[o - 1], 1)

            self.copy_z(q, o).start()

    def stage3(self, q):
        s = lax.rem(q, self.nz)

        @pl.when(q >= self.nz)
        def _():
            self.copy_out(q - self.nz).wait()

        for o in (1, 2, 3):
            self.copy_z(q, o).wait()
        total = self.acc[s] + self.zr[s, 0].astype(f32) + self.zr[s, 1].astype(f32) + self.zr[s, 2].astype(f32)
        total = total.astype(bf16)
        self.go[s] = total
        total = total.astype(f32)
        self.sums[...] += jnp.sum((total * total).reshape(-1, 8, total.shape[-1]), 0).reshape(8, -1, 128).sum(1)

        @pl.when(q + self.nz < self.total)
        def _():
            for o in (1, 2, 3):
                self.signal(self.cz.at[3 - o], device(self.r, self.y, lax.rem(self.z + o, 4), self.c))

        self.copy_out(q).start()

    def tick(self, t, first, count):
        for lag, stage in reversed(list(zip(self.LAGS, (self.stage0, self.stage1, self.stage2, self.stage3), strict=True))):
            q = t - lag

            @pl.when((q >= 0) & (q < count))
            def _():
                stage(first + q)

    def finish(self):
        for i in range(self.nz):
            self.copy_out(self.total - self.nz + i).wait()


class Staged:
    def __init__(self, at):
        self.at = at

    def start(self, q):
        pass

    def wait(self, q):
        pass

    def read(self, q, b):
        return self.at(q, b)[...]


class Fetched:
    def __init__(self, source, buf, sems, slots):
        self.source, self.buf, self.sems, self.slots = source, buf, sems, slots

    def copies(self, q):
        s = lax.rem(q, self.slots)
        return [pltpu.make_async_copy(src, self.buf.at[s, b], self.sems.at[s, b]) for src, b in self.source(q)]

    def start(self, q):
        for copy in self.copies(q):
            copy.start()

    def wait(self, q):
        for copy in self.copies(q):
            copy.wait()

    def read(self, q, b):
        return self.buf[lax.rem(q, self.slots), b]


B = 640
NB = FF // B
DC, DP = 256, 4
HALF = 512
EC = 256
GS, DS = (2, 3, 3), (2, 2, 2)
ES = 3
STEPS = T // EC


def backward_kernel(
    dy_ref, h1_ref, a1_ref, a0_ref, gate1, up1, gate0, up0, mid1, mid0, wg_ref, wu_ref, wd_ref,
    g_out, d_out, sums_out, dd_ref,
    sums, dh, a, da, ga, ua, dmid, dgu, wgu, wdj, dwst, ddst, xo,
    s_dh, s_a, s_gu, s_mid, s_wgu, s_wd, s_dd, s_xo, *bufs,
):
    half = len(bufs) // 2
    r, y, z, c = place()
    cp = pltpu.make_async_copy

    load_dh = cp(dy_ref, dh, s_dh)
    load_dh.start()
    load_a1 = cp(a1_ref, a, s_a)
    load_a1.start()
    greet(r, y, z, c)
    sums[...] = jnp.zeros_like(sums)
    da[...] = jnp.zeros_like(da)

    def g_part(q):
        n = q // 2
        return lax.rem(n, 2), pl.ds(pl.multiple_of(lax.rem(q, 2) * B, 128), B)

    def g_source(q, c):
        s, cols = g_part(q)
        return [(dwst.at[s, :, c, :, cols], None)]

    def g_own(q, b):
        s, cols = g_part(q)
        return dwst.at[s, b, c, :, cols]

    def g_to(q):
        n = q // 2
        return g_out.at[n // NB * 2 + lax.rem(q, 2), :, pl.ds(pl.multiple_of(lax.rem(n, NB) * B, 128), B)]

    def d_source(q, c):
        m, p = q // DP, lax.rem(q, DP)
        cols = pl.ds(pl.multiple_of(p * DC, 128), DC)
        return [(dd_ref.at[m, pl.ds((2 * b + c) * 25, 25), :, cols], b) for b in range(8)]

    def d_to(q):
        m, p = q // DP, lax.rem(q, DP)
        return d_out.at[m, :, :, pl.ds(pl.multiple_of(p * DC, 128), DC)]

    gr = Reducer(g_source, Staged(g_own), g_to, sums, GS, 4 * NB, bufs[:half])
    dr = Reducer(d_source, Fetched(lambda q: d_source(q, c), xo, s_xo, DS[0]), d_to, sums, DS, 2 * DP, bufs[half:])

    for n, (gate, up, mid) in enumerate(((gate1, up1, mid1), (gate0, up0, mid0))):
        layer = 1 - n

        def load_mid(st):
            s = lax.rem(st, 2)
            return cp(mid.at[:, pl.ds(pl.multiple_of(lax.rem(st, NB) * B, 128), B)],
                      dgu.at[:, pl.ds(pl.multiple_of(s * B, 128), B)], s_mid.at[s])

        def write_dd(st):
            return cp(ddst.at[lax.rem(st, 2)],
                      dd_ref.at[n, pl.ds(lax.rem(st, NB) * (B // 8), B // 8), :, pl.ds(pl.multiple_of(st // NB * HALF, 128), HALF)],
                      s_dd.at[lax.rem(st, 2)])

        def load_wd(j):
            s = lax.rem(j, 2)
            return cp(wd_ref.at[layer, pl.ds(pl.multiple_of(j * B, 8), B)], wdj.at[s], s_wd.at[s])

        def load_wgu(j):
            cols = pl.ds(pl.multiple_of(j * B, 128), B)
            return cp(wg_ref.at[layer, :, cols], wgu.at[:, pl.ds(0, B)], s_wgu.at[0]), cp(wu_ref.at[layer, :, cols], wgu.at[:, pl.ds(B, B)], s_wgu.at[1])

        def load_gu(k):
            s, j, i = lax.rem(k, ES), k // STEPS, lax.rem(k, STEPS)
            at = (pl.ds(pl.multiple_of(i * EC, 8), EC), pl.ds(pl.multiple_of(j * B, 128), B))
            return cp(gate.at[at], ga.at[s], s_gu.at[s, 0]), cp(up.at[at], ua.at[s], s_gu.at[s, 1])

        load_mid(0).start()
        load_wd(0).start()
        for k in range(ES - 1):
            for copy in load_gu(k):
                copy.start()
        if n == 0:
            load_dh.wait()

        def down(st, _):
            @pl.when(st + 1 < 2 * NB)
            def _():
                load_mid(st + 1).start()

            load_mid(st).wait()
            s = lax.rem(st, 2)
            tile = dot(dgu[:, pl.ds(pl.multiple_of(s * B, 128), B)], dh[:, pl.ds(pl.multiple_of(st // NB * HALF, 128), HALF)], 0, 0)
            ddst[s] = tile.astype(bf16).reshape(B // 8, 8, HALF)

            @pl.when((st != 0) & (st != NB))
            def _():
                write_dd(st - 1).wait()

            write_dd(st).start()

            @pl.when((st == NB - 1) | (st == 2 * NB - 1))
            def _():
                write_dd(st).wait()

            @pl.when((st == 4) | (st == 6) | (st == 9))
            def _():
                dr.tick((st - 4) // 2, n * DP, DP)

            if n == 1:

                @pl.when(lax.rem(st, 2) == 0)
                def _():
                    gr.tick(10 + st // 2, 0, 2 * NB)

            return 0

        lax.fori_loop(0, 2 * NB, down, 0)

        if n == 0:
            load_a1.wait()
        else:
            cp(a0_ref, a, s_a).wait()

        def block(j, _):
            @pl.when(j + 1 < NB)
            def _():
                load_wd(j + 1).start()

            if n == 0:
                for copy in load_wgu(j):
                    copy.start()
            load_wd(j).wait()

            def dmids(i, _):
                rows = pl.ds(pl.multiple_of(i * 512, 8), 512)
                dmid[rows, :] = dot(dh[rows, :], wdj[lax.rem(j, 2)], 1, 1).astype(bf16)
                return 0

            lax.fori_loop(0, T // 512, dmids, 0)

            def act(i, _):
                k = j * STEPS + i

                @pl.when(k + ES - 1 < NB * STEPS)
                def _():
                    for copy in load_gu(k + ES - 1):
                        copy.start()

                for copy in load_gu(k):
                    copy.wait()
                s = lax.rem(k, ES)
                rows = pl.ds(pl.multiple_of(i * EC, 8), EC)
                dm = dmid[rows, :].astype(f32)
                ge = ga[s]
                sig = 0.5 + 0.5 * jnp.tanh(0.5 * ge)
                silu = ge * sig
                dgu[rows, 0:B] = (dm * ua[s] * (sig + silu * (1.0 - sig))).astype(bf16)
                dgu[rows, B : 2 * B] = (dm * silu).astype(bf16)
                return 0

            lax.fori_loop(0, STEPS, act, 0)

            dr.tick(3 + 2 * j, n * DP, DP)

            @pl.when(j >= 1)
            def _():
                gr.tick(2 * j - 1, n * 2 * NB, 2 * NB)

            def terms(i, _):
                rows = pl.ds(pl.multiple_of(i * 512, 128), 512)
                dwst[lax.rem(n * NB + j, 2), pl.ds(i * 4, 4)] = dot(a[:, rows], dgu[...], 0, 0).astype(bf16).reshape(4, 2, 64, 2 * B)
                return 0

            lax.fori_loop(0, D // 512, terms, 0)

            dr.tick(4 + 2 * j, n * DP, DP)
            gr.tick(2 * j, n * 2 * NB, 2 * NB)

            if n == 0:
                for copy in load_wgu(j):
                    copy.wait()

                def back(i, _):
                    rows = pl.ds(pl.multiple_of(i * 512, 8), 512)
                    da[rows, :] += dot(dgu[rows, :], wgu[...], 1, 1)
                    return 0

                lax.fori_loop(0, T // 512, back, 0)
            return 0

        lax.fori_loop(0, NB, block, 0)
        gr.tick(9, n * 2 * NB, 2 * NB)
        if n == 0:
            load_h = cp(h1_ref, a, s_a)
            load_h.start()
            load_h.wait()

            def norm(i, _):
                rows = pl.ds(pl.multiple_of(i * 128, 8), 128)
                wide = a[rows, :].astype(f32)
                d = da[rows, :].astype(bf16).astype(f32)
                scale = lax.rsqrt(jnp.mean(wide * wide, -1, keepdims=True) + 1e-6)
                inner = jnp.mean(d * wide, -1, keepdims=True)
                dn = (scale * d - wide * (scale * scale * scale * inner)).astype(bf16)
                dh[rows, :] = (dh[rows, :].astype(f32) + dn.astype(f32)).astype(bf16)
                return 0

            lax.fori_loop(0, T // 128, norm, 0)
            load_a0 = cp(a0_ref, a, s_a)
            load_a0.start()

    lax.fori_loop(10, 15, lambda t, _: (gr.tick(t, 2 * NB, 2 * NB), 0)[1], 0)
    dr.finish()
    gr.finish()
    sums_out[...] = sums[...]


def backward(dy, h1, a1, a0, gate1, up1, gate0, up0, mid1, mid0, wg, wu, wd):
    V, dma = pltpu.VMEM, pltpu.SemaphoreType.DMA
    return pl.pallas_call(
        backward_kernel,
        out_shape=(
            jax.ShapeDtypeStruct((4, 64, FF), bf16),
            jax.ShapeDtypeStruct((2, 25, 8, D), bf16),
            jax.ShapeDtypeStruct((8, 128), f32),
            jax.ShapeDtypeStruct((2, FF // 8, 8, D), bf16),
        ),
        in_specs=[pl.BlockSpec(memory_space=HBM)] * 13,
        out_specs=(pl.BlockSpec(memory_space=HBM), pl.BlockSpec(memory_space=HBM), pl.BlockSpec(memory_space=V), pl.BlockSpec(memory_space=HBM)),
        scratch_shapes=[
            V((8, 128), f32), V((T, D), bf16), V((T, D), bf16), V((T, D), f32), V((ES, EC, B), f32), V((ES, EC, B), f32),
            V((T, B), bf16), V((T, 2 * B), bf16), V((D, 2 * B), bf16), V((2, B, D), bf16), V((2, 8, 2, 64, 2 * B), bf16),
            V((2, B // 8, 8, HALF), bf16), V((DS[0], 8, 25, 8, DC), bf16),
            dma, dma, dma((ES, 2)), dma((2,)), dma((2,)), dma((2,)), dma((2,)), dma((DS[0], 8)),
        ] + Reducer.scratch((64, B), 1, GS) + Reducer.scratch((25, 8, DC), 8, DS),
        compiler_params=pltpu.CompilerParams(collective_id=0, has_side_effects=True, vmem_limit_bytes=67043328),
    )(dy, h1, a1, a0, gate1, up1, gate0, up0, mid1, mid0, wg, wu, wd)


def gather_kernel(sg, su, sd, og, ou, od, zs, zr, ys, yr, ds, dr, ls):
    r, y, z, c = place()
    greet(r, y, z, c)
    chunks = [(s, o, layer) for layer in range(2) for s, o in ((sg, og), (su, ou), (sd, od))]
    n = len(chunks)

    def block(y, z, c):
        return y * 8 + z * 2 + c

    def zat(o):
        return lax.rem(z + o, 4)

    partner, across = device(r, y, z, 1 - c), device(r, 1 - y, z, c)
    mine = block(y, z, c)
    sent = []

    def send(src, k, b, ssem, rsem, dev):
        _, o, layer = chunks[k]
        copy = pltpu.make_async_remote_copy(src, o.at[layer, b], ssem, rsem, device_id=dev, device_id_type=MESH)
        copy.start()
        sent.append(copy)

    def arrived(k, b, ssem, rsem, dev):
        _, o, layer = chunks[k]
        ref = o.at[layer, b]
        pltpu.make_async_remote_copy(ref, ref, ssem, rsem, device_id=dev, device_id_type=MESH).wait_recv()
        return ref

    local = []
    for k, (s, o, layer) in enumerate(chunks):
        for d in (1, 2, 3):
            send(s.at[layer], k, mine, zs.at[k, d - 1], zr.at[k, 3 - d], device(r, y, zat(d), c))
        send(s.at[layer], k, mine, ys.at[k, 0], yr.at[k, 0], across)
        send(s.at[layer], k, mine, ds.at[k, 0], dr.at[k, 0], partner)
        copy = pltpu.make_async_copy(s.at[layer], o.at[layer, mine], ls.at[k])
        copy.start()
        local.append(copy)
    for k in range(n + 1):
        if k < n:
            for d in (1, 2, 3):
                b = block(y, zat(d), c)
                ref = arrived(k, b, zs.at[k, d - 1], zr.at[k, d - 1], across)
                send(ref, k, b, ys.at[k, d], yr.at[k, d], across)
                send(ref, k, b, ds.at[k, d], dr.at[k, d], partner)
        if k >= 1:
            for d in range(4):
                b = block(1 - y, zat(d), c)
                ref = arrived(k - 1, b, ys.at[k - 1, d], yr.at[k - 1, d], across)
                send(ref, k - 1, b, ds.at[k - 1, 4 + d], dr.at[k - 1, 4 + d], partner)
    for k in range(n):
        for e in range(8):
            b = block(y if e < 4 else 1 - y, zat(e % 4), 1 - c)
            arrived(k, b, ds.at[k, e], dr.at[k, e], partner)
    for copy in sent:
        copy.wait_send()
    for copy in local:
        copy.wait()


def all_gather(sg, su, sd):
    dma = pltpu.SemaphoreType.DMA
    out = pl.pallas_call(
        gather_kernel,
        out_shape=(
            jax.ShapeDtypeStruct((2, 16, 64, FF), bf16),
            jax.ShapeDtypeStruct((2, 16, 64, FF), bf16),
            jax.ShapeDtypeStruct((2, 16, 200, D), bf16),
        ),
        in_specs=[pl.BlockSpec(memory_space=pltpu.VMEM)] * 3,
        out_specs=[pl.BlockSpec(memory_space=HBM)] * 3,
        scratch_shapes=[dma((6, 3)), dma((6, 3)), dma((6, 4)), dma((6, 4)), dma((6, 8)), dma((6, 8)), dma((6,))],
        compiler_params=pltpu.CompilerParams(collective_id=1, has_side_effects=True),
    )(sg, su, sd)
    return out[0].reshape(2, D, FF), out[1].reshape(2, D, FF), out[2].reshape(2, FF, D)


def normed(h):
    wide = h.astype(f32)
    return (wide * lax.rsqrt(jnp.mean(wide**2, -1, keepdims=True) + 1e-6)).astype(bf16)


def forward(x, wg, wu, wd):
    h, kept = x, []
    for i in range(2):
        a = normed(h)
        gate, up = dot(a, wg[i], 1, 0), dot(a, wu[i], 1, 0)
        mid = (jax.nn.silu(gate) * up).astype(bf16)
        kept.append((a, gate, up, mid))
        if i == 0:
            h = h + dot(mid, wd[i], 1, 0).astype(bf16)
    return h, *kept


def adamw(w, m, v, g):
    m = 0.9 * m + 0.1 * g
    v = 0.95 * v + 0.05 * g * g
    step = m * lax.rsqrt(v + 1e-8) + 0.1 * w
    return (w - 0.02 * step).astype(bf16), m, v


def solution(mesh):
    def step(x, dy, wg, wu, wd, mg, mu, md, vg, vu, vd):
        h1, (a0, gate0, up0, mid0), (a1, gate1, up1, mid1) = forward(x[0], wg, wu, wd)
        gg, gd, sums, _ = backward(dy[0], h1, a1, a0, gate1, up1, gate0, up0, mid1, mid0, wg, wu, wd)
        gd = gd.reshape(2, 200, D)
        squares = lax.psum(jnp.sum(sums), "dp")
        factor = jnp.minimum(1.0, 0.5 * lax.rsqrt(squares / (6 * D * FF) + 1e-30))
        me = lax.axis_index("dp")
        new = []
        for w, m, v, g in ((wg, mg, vg, gg[2::-2]), (wu, mu, vu, gg[3::-2]), (wd, md, vd, gd[::-1])):
            rows = m.shape[1]
            mine = lax.dynamic_slice_in_dim(w, me * rows, rows, 1)
            new.append(adamw(mine.astype(f32), m, v, g.astype(f32) * factor))
        weights = all_gather(*(n[0] for n in new))
        return (*weights, *(n[1] for n in new), *(n[2] for n in new))

    seq, rep, own = P(("rep", "dp")), P("rep"), P("rep", "dp")
    return jax.shard_map(
        step,
        mesh=mesh,
        in_specs=(seq, seq, P(), P(), P(), *[P(None, "dp")] * 6),
        out_specs=(rep,) * 3 + (own,) * 6,
        check_vma=False,
    )
```

time: 1060 us -> 786 us (0.74)
  matrix products: 371 us -> 125 us
  other arithmetic: 47.4 us -> 21 us
    dot_general x15 -> x5, matrix products: 371 us -> 125 us  [dot(): lax.dot_general(a, b, (((ca,), (cb,)), ((), ())), preferred_element_type=...]
    another operation x2 -> x0, other arithmetic: 24.2 us -> none  [local_terms(): return (jnp.stack([dwg1, dwu1, dwg0, dwu0]), jnp.stack([dwd1, dwd0]))]
    pallas_call x1, Pallas kernels: 282 us -> 293 us  [backward(): pl.pallas_call(backward_kernel, out_shape=(jax.ShapeDtypeStruct((4, 64, F...]
    unnamed x39 -> x23, local copies, waits for them, and re-layouts: 40.3 us -> 30.1 us
where the time goes in v2:
time: 786 us; the launch traced here: 777 us
  Pallas kernels  570 us (73%)
  matrix products  125 us (16%)
  local copies, waits for them, and re-layouts  30.3 us (4%)
  blocking collectives  29.2 us (4%)
  other arithmetic  21 us (3%)
    pallas_call x1, Pallas kernels, backward(): pl.pallas_call(backward_kernel, out_shape=(jax.ShapeDtypeStruct((4, 64, F...  293 us
    pallas_call x1, Pallas kernels, all_gather(): pl.pallas_call(gather_kernel, out_shape=(jax.ShapeDtypeStruct((2, 16, 64,...  276 us
    dot_general x5, matrix products, dot(): lax.dot_general(a, b, (((ca,), (cb,)), ((), ())), preferred_element_type=...  125 us
    unnamed x23, local copies, waits for them, and re-layouts  30.1 us
    psum x1, blocking collectives, step(): squares = lax.psum(jnp.sum(sums), 'dp')  29.2 us

profile of v2, /device:TPU:11, one launch (start us, length us, event | category | flops | bytes accessed | tf_op | source)
XLA Modules:
  0.0 776.6 jit_solution(9318159820129296208)
XLA Ops:
  0.6 0.0 copy-start.2
  0.7 3.2 fusion
  3.9 0.2 copy-done.2
  4.1 20.9 %fusion.12.gate0 = f32[2048,3200]{1,0:T(8,128)} fusion(bf16[2,1024,3200]{2,1,0:T(8,128)(2,1)} %wg_ref.1, bf16[1,2048,1024]{2,1,0:T(8,128)(2,1)S(1)} %copy-done.2, f32[2048]{0:T(1024)S(1)} %add_rsqrt_fusion.1), kind=kOutput, calls=%fused_computation.19 | convolution fusion | flops 13428064256 | bytes 36970496 | tf_op jit(solution)/shard_map/dot_general | solution.py:34
  25.0 32.1 %multiply_convert_fusion.1 = (bf16[2048,3200]{1,0:T(8,128)(2,1)}, f32[2048,3200]{1,0:T(8,128)}) fusion(f32[2048,3200]{1,0:T(8,128)} %fusion.12.gate0, bf16[2,1024,3200]{2,1,0:T(8,128)(2,1)} %wu_ref.1, bf16[1,2048,1024]{2,1,0:T(8,128)(2,1)} %param.11, f32[2048]{0:T(1024)S(1)} %add_rsqrt_fusion.1), kind=kOutput, calls=%fused_computation.1 | convolution fusion | flops 13467385856 | bytes 76292096 | tf_op jit(solution)/shard_map/dot_general | solution.py:34
  57.1 19.4 %fusion.2 = (f32[2048]{0:T(1024)S(1)}, bf16[2048,1024]{1,0:T(8,128)(2,1)S(1)}) fusion(bf16[2048,3200]{1,0:T(8,128)(2,1)} %get-tuple-element.32.mid0, bf16[2,3200,1024]{2,1,0:T(8,128)(2,1)} %wd_ref.1, bf16[1,2048,1024]{2,1,0:T(8,128)(2,1)} %param.11), kind=kOutput, calls=%fused_computation.8 | convolution fusion | flops 13432256512 | bytes 28057600 | tf_op jit(solution)/shard_map/dot_general | solution.py:34
  76.5 0.0 copy-start
  76.5 0.7 fusion.3.a1_ref
  77.3 1.2 copy-done
  78.5 0.0 copy-start.1
  78.5 2.0 copy-done.1
  80.5 20.5 %fusion.6.gate1 = f32[2048,3200]{1,0:T(8,128)} fusion(bf16[2048,1024]{1,0:T(8,128)(2,1)S(1)} %fusion.3.a1_ref, bf16[2,1024,3200]{2,1,0:T(8,128)(2,1)} %wg_ref.1), kind=kOutput, calls=%fused_computation.13 | convolution fusion | flops 13421772800 | bytes 36962304 | tf_op jit(solution)/shard_map/dot_general | solution.py:34
  101.0 31.8 %multiply_convert_fusion = (bf16[2048,3200]{1,0:T(8,128)(2,1)}, f32[2048,3200]{1,0:T(8,128)}) fusion(f32[2048,3200]{1,0:T(8,128)} %fusion.6.gate1, bf16[2048,1024]{1,0:T(8,128)(2,1)} %copy-done.1, bf16[2,1024,3200]{2,1,0:T(8,128)(2,1)} %wu_ref.1), kind=kOutput, calls=%fused_computation | convolution fusion | flops 13461094400 | bytes 76283904 | tf_op jit(solution)/shard_map/dot_general | solution.py:34
  132.8 5.0 fusion.1.a0_ref
  137.8 293.4 %shard_map.178 = (bf16[4,64,3200]{2,1,0:T(8,128)(2,1)}, bf16[2,25,8,1024]{3,2,1,0:T(8,128)(2,1)}, f32[8,128]{1,0:T(8,128)}, bf16[2,400,8,1024]{3,2,1,0:T(8,128)(2,1)}) custom-call(bf16[2048,1024]{1,0:T(8,128)(2,1)} %bitcast.46, bf16[2048,1024]{1,0:T(8,128)(2,1)} %copy-done, bf16[2048,1024]{1,0:T(8,128)(2,1)} %copy-done.1, bf16[2048,1024]{1,0:T(8,128)(2,1)} %fusion.1.a0_ref, ...), custom_call_target="tpu_custom_call" | custom-call | tf_op jit(solution)/shard_map/pallas_call | solution.py:433
  431.2 1.3 reduce_sum.29
  432.5 29.2 %psum.7 = f32[]{:T(128)} all-reduce(f32[]{:T(128)} %reduce_sum.29), channel_id=1, replica_groups=mesh['rep'=2,'dp'=16] {'dp'}, use_global_device_ids=true, to_apply=%region_3.4 | all-reduce | flops 1 | bytes 8 | tf_op jit(solution)/shard_map/psum | solution.py:558
  462.4 0.0 copy-start.5
  462.4 0.0 copy-start.4
  462.4 5.2 fusion.32
  467.6 0.0 copy-done.5
  467.6 0.1 fusion.39
  467.7 0.0 copy-done.4
  467.7 5.6 fusion.26
  473.2 276.1 %shard_map.179 = (bf16[2,16,64,3200]{3,2,1,0:T(8,128)(2,1)}, bf16[2,16,64,3200]{3,2,1,0:T(8,128)(2,1)}, bf16[2,16,200,1024]{3,2,1,0:T(8,128)(2,1)}) custom-call(bf16[2,64,3200]{2,1,0:T(8,128)(2,1)} %get-tuple-element.27.sg, bf16[2,64,3200]{2,1,0:T(8,128)(2,1)} %get-tuple-element.38.su, bf16[2,200,1024]{2,1,0:T(8,128)(2,1)} %get-tuple-element.21.sd), custom_call_target="tpu_custom_call" | custom-call | tf_op jit(solution)/shard_map/pallas_call | solution.py:514
  749.4 0.0 copy-start.3
  749.4 0.0 slice-start
  749.4 0.0 slice-start.1
  749.4 12.7 %copy.25 = bf16[2,1024,3200]{2,1,0:T(8,128)(2,1)} copy(bf16[2,1024,3200]{2,1,0:T(8,128)(2,1)} %bitcast.45) | data formatting | bytes 26214400
  762.1 0.0 copy-done.3
  762.1 0.0 slice-start.2
  762.1 0.0 slice-start.3
  762.1 6.6 copy.26
  768.7 0.0 slice-done
  768.7 1.2 slice-done.1
  769.9 1.3 slice-done.2
  771.2 0.0 slice-done.3
  771.2 4.9 copy.27
  (3 shorter events, 0.0 us)
Async XLA Ops:
  0.6 3.5 copy-start.2
  76.5 2.0 copy-start
  78.5 2.0 copy-start.1
  462.4 5.2 copy-start.5
  462.4 5.3 copy-start.4
  749.4 12.7 %copy-start.3 = (bf16[2,16,64,3200]{3,2,1,0:T(8,128)(2,1)S(1)}, bf16[2,16,64,3200]{3,2,1,0:T(8,128)(2,1)}, u32[]{:S(2)}) copy-start(bf16[2,16,64,3200]{3,2,1,0:T(8,128)(2,1)} %get-tuple-element.19) | copy-start | bytes 39321604
  749.4 19.4 %slice-start = ((s8[13107200]{0:T(1024)(128)(4,1)}), s8[4194304]{0:T(1024)(128)(4,1)S(1)}, s32[]{:S(2)}) async-start(s8[13107200]{0:T(1024)(128)(4,1)} %bitcast.41), calls=%async_computation | async-start | bytes 8388608
  749.4 20.5 %slice-start.1 = ((s8[13107200]{0:T(1024)(128)(4,1)}), s8[4194304]{0:T(1024)(128)(4,1)S(1)}, s32[]{:S(2)}) async-start(s8[13107200]{0:T(1024)(128)(4,1)} %bitcast.41), calls=%async_computation.1 | async-start | bytes 8388608
  762.1 9.1 %slice-start.2 = ((s8[13107200]{0:T(1024)(128)(4,1)}), s8[4194304]{0:T(1024)(128)(4,1)S(1)}, s32[]{:S(2)}) async-start(s8[13107200]{0:T(1024)(128)(4,1)} %bitcast.41), calls=%async_computation.2 | async-start | bytes 8388608
  762.1 9.1 %slice-start.3 = ((s8[13107200]{0:T(1024)(128)(4,1)}), s8[524288]{0:T(1024)(128)(4,1)S(1)}, s32[]{:S(2)}) async-start(s8[13107200]{0:T(1024)(128)(4,1)} %bitcast.41), calls=%async_computation.3 | async-start | bytes 1048576

commit v3 on v0

v3 whole, which is shorter than its diff:
```python
import functools

import jax
import jax.numpy as jnp
from jax import lax
from jax.experimental import pallas as pl
from jax.experimental.pallas import tpu as pltpu
from jax.sharding import PartitionSpec as P

MESH = pl.DeviceIdType.MESH
HBM, VMEM = pltpu.HBM, pltpu.VMEM
DMA, REGULAR = pltpu.SemaphoreType.DMA, pltpu.SemaphoreType.REGULAR
bf16, f32 = jnp.bfloat16, jnp.float32
D, FF, T = 1024, 3200, 2048
B = 640
NB = FF // B
R = 512
ring = lax.rem


def place():
    me = lax.axis_index("dp")
    return lax.axis_index("rep"), me // 8, ring(me // 2, 4), ring(me, 2)


def device(r, y, z, c):
    return (r, y * 8 + z * 2 + c)


def greet(r, y, z, c):
    bar = pltpu.get_barrier_semaphore()
    peers = [device(r, y, z, 1 - c), device(r, 1 - y, z, c)] + [device(r, y, ring(z + o, 4), c) for o in (1, 2, 3)]
    for p in peers:
        signal(bar, p)
    pl.semaphore_wait(bar, len(peers))


def signal(sem, dev):
    pl.semaphore_signal(sem, 1, device_id=dev, device_id_type=MESH)


def remote(src, dst, ssem, rsem, dev):
    return pltpu.make_async_remote_copy(src, dst, ssem, rsem, device_id=dev, device_id_type=MESH)


def start(copies):
    for copy in copies:
        copy.start()


def finish(copies):
    for copy in copies:
        copy.wait()


def loop(n, body):
    lax.fori_loop(0, n, lambda i, carry: (body(i), carry)[1], None)


def when(ok):
    return pl.when(ok)


def part(i, n):
    return pl.ds(pl.multiple_of(i * n, n), n)


def dot(a, b, ca, cb):
    return lax.dot_general(a, b, (((ca,), (cb,)), ((), ())), preferred_element_type=f32)


nn = functools.partial(dot, ca=1, cb=0)
nt = functools.partial(dot, ca=1, cb=1)
tn = functools.partial(dot, ca=0, cb=0)


def normed(h):
    wide = h.astype(f32)
    return (wide * lax.rsqrt(jnp.mean(wide * wide, -1, keepdims=True) + 1e-6)).astype(bf16)


N = 128
CHUNKS = T // R
STEPS = NB * CHUNKS
FS = 4


def forward_kernel(
    x_ref, wg_ref, wu_ref, wd_ref,
    a0_ref, a1_ref, h1_ref, p0, s0, m0, p1, s1, m1,
    x, a, total, wgu, wdj, g, stp, sts, sta, stb, s_x, s_out, s_wg, s_wu, s_wd, s_p, s_s, s_m,
):
    cp = pltpu.make_async_copy

    def load_w(n):
        s, cols = ring(n, 2), part(ring(n, NB), B)
        return (cp(wg_ref.at[n // NB, :, cols], wgu.at[s, :, pl.ds(0, B)], s_wg.at[s]),
                cp(wu_ref.at[n // NB, :, cols], wgu.at[s, :, pl.ds(B, B)], s_wu.at[s]))

    def load_wd(j):
        s = ring(j, 2)
        return cp(wd_ref.at[0, part(j, B)], wdj.at[s], s_wd.at[s])

    load_x = cp(x_ref, x, s_x)
    load_x.start()
    start(load_w(0))
    total[...] = jnp.zeros_like(total)
    stb[...] = jnp.zeros_like(stb)
    load_wd(0).start()
    load_x.wait()

    def norm(i):
        rows = part(i, N)
        a[rows, :] = normed(x[rows, :])

    loop(T // N, norm)
    out_a0 = cp(a, a0_ref, s_out.at[0])
    out_a0.start()
    load_wd(0).wait()
    for layer, (p, s, m) in enumerate(((p0, s0, m0), (p1, s1, m1))):

        def writes(k, even):
            t, u, at = ring(k, FS), ring(k // 2, FS // 2), (part(ring(k, CHUNKS), R), part(k // CHUNKS, B))
            return cp(stp.at[t], p.at[at], s_p.at[t]), cp(sts.at[t], s.at[at], s_s.at[t]), cp((sta if even else stb).at[u], m.at[at], s_m.at[t])

        def down(k, even):
            mid = (sta if even else stb)[ring(k // 2, FS // 2)]
            total[part(ring(k, CHUNKS), R), :] += nn(mid, wdj[ring(k // CHUNKS, 2)])

        def step(k, even):
            j, i, t = k // CHUNKS, ring(k, CHUNKS), ring(k, FS)
            n = layer * NB + j

            @when(i == 0)
            def _():
                finish(load_w(n))

                @when(n + 1 < 2 * NB)
                def _():
                    start(load_w(n + 1))

            if layer == 0:

                @when(i == 1)
                def _():
                    @when(j > 0)
                    def _():
                        load_wd(j).wait()

                    @when(j + 1 < NB)
                    def _():
                        load_wd(j + 1).start()

            @when(k >= FS)
            def _():
                finish(writes(k - FS, even))

            g[...] = nn(a[part(i, R), :], wgu[ring(n, 2)])
            if layer == 0:
                down(jnp.where(k == 0, STEPS - 1, k - 1), not even)
            gate, up = g[:, :B], g[:, B:]
            sig = 0.5 + 0.5 * jnp.tanh(0.5 * gate)
            silu = gate * sig
            (sta if even else stb)[ring(k // 2, FS // 2)] = (silu * up).astype(bf16)
            stp[t] = up * (sig + silu * (1.0 - sig))
            sts[t] = silu
            start(writes(k, even))

        def steps(i):
            step(2 * i, True)
            step(2 * i + 1, False)

        loop(STEPS // 2, steps)
        if layer == 0:
            down(STEPS - 1, False)
        for k in range(STEPS - FS, STEPS):
            finish(writes(k, k % 2 == 0))
        if layer == 0:
            out_a0.wait()
            def joint(i):
                rows = part(i, N)
                h = (x[rows, :].astype(f32) + total[rows, :].astype(bf16).astype(f32)).astype(bf16)
                x[rows, :] = h
                a[rows, :] = normed(h)

            loop(T // N, joint)
            outs = cp(x, h1_ref, s_out.at[0]), cp(a, a1_ref, s_out.at[1])
            start(outs)
    finish(outs)


def forward(x, wg, wu, wd):
    states, wide, mid = (jax.ShapeDtypeStruct((T, n), t) for n, t in ((D, bf16), (FF, f32), (FF, bf16)))
    two = (2,)
    return pl.pallas_call(
        forward_kernel,
        out_shape=(states,) * 3 + (wide, wide, mid) * 2,
        in_specs=[pl.BlockSpec(memory_space=HBM)] * 4,
        out_specs=(pl.BlockSpec(memory_space=HBM),) * 9,
        scratch_shapes=[
            VMEM((T, D), bf16), VMEM((T, D), bf16), VMEM((T, D), f32), VMEM((2, D, 2 * B), bf16), VMEM((2, B, D), bf16),
            VMEM((R, 2 * B), f32), VMEM((FS, R, B), f32), VMEM((FS, R, B), f32), VMEM((FS // 2, R, B), bf16), VMEM((FS // 2, R, B), bf16),
            DMA, DMA(two), DMA(two), DMA(two), DMA(two), DMA((FS,)), DMA((FS,)), DMA((FS,)),
        ],
        compiler_params=pltpu.CompilerParams(vmem_limit_bytes=67043328),
    )(x, wg, wu, wd)


class Reducer:
    LAGS = (0, 1, 3, 5)

    def __init__(self, source, own, out, sums, slots, total, bufs):
        self.source, self.own, self.out, self.sums, self.total = source, own, out, sums, total
        self.nx, self.ny, self.nz = slots
        (self.xr, self.ys, self.yr, self.s1, self.acc, self.zs, self.zr, self.go,
         self.xss, self.xrs, self.yss, self.yrs, self.zss, self.zrs, self.gos, self.cx, self.cy, self.cz) = bufs
        r, y, self.z, c = place()
        self.y, self.c = y, c
        self.partner, self.across = device(r, y, self.z, 1 - c), device(r, 1 - y, self.z, c)
        self.along = [device(r, y, self.zat(o), c) for o in (1, 2, 3)]

    def zat(self, o):
        return ring(self.z + o, 4)

    @staticmethod
    def scratch(shape, parts, slots):
        nx, ny, nz = slots
        return [
            VMEM((nx, 8, *shape), bf16), VMEM((ny, 4, *shape), bf16), VMEM((ny, 4, *shape), bf16), VMEM((ny, 4, *shape), f32),
            VMEM((nz, *shape), f32), VMEM((nz, 3, *shape), bf16), VMEM((nz, 3, *shape), bf16), VMEM((nz, *shape), bf16),
            DMA((nx, parts)), DMA((nx, parts)), DMA((ny,)), DMA((ny,)), DMA((nz, 3)), DMA((nz, 3)), DMA((nz,)), REGULAR, REGULAR, REGULAR((3,)),
        ]

    def copies_x(self, q):
        s = ring(q, self.nx)
        return [
            remote(src, self.xr.at[s] if b is None else self.xr.at[s, b], self.xss.at[s, b or 0], self.xrs.at[s, b or 0], self.partner)
            for src, b in self.source(q, 1 - self.c)
        ]

    def copy_y(self, q):
        s = ring(q, self.ny)
        return remote(self.ys.at[s], self.yr.at[s], self.yss.at[s], self.yrs.at[s], self.across)

    def copies_z(self, q):
        s = ring(q, self.nz)
        return [remote(self.zs.at[s, i], self.zr.at[s, 2 - i], self.zss.at[s, i], self.zrs.at[s, 2 - i], dev) for i, dev in enumerate(self.along)]

    def copy_out(self, q):
        s = ring(q, self.nz)
        return pltpu.make_async_copy(self.go.at[s], self.out(q), self.gos.at[s])

    def stage0(self, q):
        @when(q >= self.nx)
        def _():
            pl.semaphore_wait(self.cx, 1)

        start(self.copies_x(q))
        self.own.start(q)

    def stage1(self, q):
        x, s = ring(q, self.nx), ring(q, self.ny)
        self.own.wait(q)
        finish(self.copies_x(q))

        def add(i):
            b = (1 - self.y) * 4 + i
            self.ys[s, i] = (self.own.read(q, b).astype(f32) + self.xr[x, b].astype(f32)).astype(bf16)
            b = self.y * 4 + i
            self.s1[s, i] = self.own.read(q, b).astype(f32) + self.xr[x, b].astype(f32)

        loop(4, add)

        @when(q + self.nx < self.total)
        def _():
            signal(self.cx, self.partner)

        @when(q >= self.ny)
        def _():
            pl.semaphore_wait(self.cy, 1)

        self.copy_y(q).start()

    def stage2(self, q):
        s, t = ring(q, self.ny), ring(q, self.nz)
        self.copy_y(q).wait()
        for i in range(3):
            b = self.zat(i + 1)
            self.zs[t, i] = (self.s1[s, b] + self.yr[s, b].astype(f32)).astype(bf16)
        self.acc[t] = self.s1[s, self.z] + self.yr[s, self.z].astype(f32)

        @when(q + self.ny < self.total)
        def _():
            signal(self.cy, self.across)

        @when(q >= self.nz)
        def _():
            for i in range(3):
                pl.semaphore_wait(self.cz.at[i], 1)

        start(self.copies_z(q))

    def stage3(self, q):
        s = ring(q, self.nz)

        @when(q >= self.nz)
        def _():
            self.copy_out(q - self.nz).wait()

        finish(self.copies_z(q))
        total = self.acc[s]
        for i in range(3):
            total += self.zr[s, i].astype(f32)
        total = total.astype(bf16)
        self.go[s] = total
        total = total.astype(f32)
        self.sums[...] += jnp.sum((total * total).reshape(-1, 8, total.shape[-1]), 0).reshape(8, -1, 128).sum(1)

        @when(q + self.nz < self.total)
        def _():
            for i, dev in enumerate(self.along):
                signal(self.cz.at[2 - i], dev)

        self.copy_out(q).start()

    def tick(self, t, first, count):
        for lag, stage in zip(self.LAGS[::-1], (self.stage3, self.stage2, self.stage1, self.stage0), strict=True):
            q = t - lag
            when((q >= 0) & (q < count))(functools.partial(stage, first + q))

    def close(self):
        finish([self.copy_out(self.total - self.nz + i) for i in range(self.nz)])


class Staged:
    def __init__(self, at):
        self.at = at

    def start(self, q):
        pass

    wait = start

    def read(self, q, b):
        return self.at(q, b)[...]


class Fetched:
    def __init__(self, source, buf, sems, slots):
        self.source, self.buf, self.sems, self.slots = source, buf, sems, slots

    def copies(self, q):
        s = ring(q, self.slots)
        return [pltpu.make_async_copy(src, self.buf.at[s, b], self.sems.at[s, b]) for src, b in self.source(q)]

    def start(self, q):
        start(self.copies(q))

    def wait(self, q):
        finish(self.copies(q))

    def read(self, q, b):
        return self.buf[ring(q, self.slots), b]


DC, DP = 256, 4
GP = 2 * NB
HALF = 512
GS, DS = (2, 3, 3), (2, 2, 2)
EC, ES = 256, 6
E = T // EC
ROWS = B // 8


def backward_kernel(
    dy_ref, h1_ref, a1_ref, a0_ref, p1, s1, mid1, p0, s0, mid0, wg_ref, wu_ref, wd_ref,
    g_out, d_out, sums_out, dd_ref,
    sums, dh, a, da, pa, sa, dgu, wgu, wdj, dwst, ddst, xo,
    tot, got, s_tot, s_tot_in, s_dh, s_a, s_ps, s_mid, s_wgu, s_wd, s_dd, s_xo, *bufs,
):
    half = len(bufs) // 2
    r, y, z, c = place()
    cp = pltpu.make_async_copy

    load_dh = cp(dy_ref, dh, s_dh)
    load_a = cp(a1_ref, a, s_a)
    load_h, load_a0 = cp(h1_ref, a, s_a), cp(a0_ref, a, s_a)
    load_dh.start()
    load_a.start()
    greet(r, y, z, c)
    sums[...] = jnp.zeros_like(sums)
    da[...] = jnp.zeros_like(da)

    def g_part(q):
        return ring(q // 2, 2), part(ring(q, 2), B)

    def g_source(q, c):
        s, cols = g_part(q)
        return [(dwst.at[s, :, c, :, cols], None)]

    def g_own(q, b):
        s, cols = g_part(q)
        return dwst.at[s, b, c, :, cols]

    def g_to(q):
        n = q // 2
        return g_out.at[ring(q, 2), 1 - n // NB, :, part(ring(n, NB), B)]

    def d_source(q, c):
        return [(dd_ref.at[q // DP, pl.ds((2 * b + c) * 25, 25), :, part(ring(q, DP), DC)], b) for b in range(8)]

    def d_to(q):
        return d_out.at[1 - q // DP, :, :, part(ring(q, DP), DC)]

    gr = Reducer(g_source, Staged(g_own), g_to, sums, GS, 2 * GP, bufs[:half])
    dr = Reducer(d_source, Fetched(lambda q: d_source(q, c), xo, s_xo, DS[0]), d_to, sums, DS, 2 * DP, bufs[half:])

    for n, (p, s, mid) in enumerate(((p1, s1, mid1), (p0, s0, mid0))):
        layer, d_first, g_first = 1 - n, n * DP, n * GP

        def load_mid(st):
            t = ring(st, 2)
            return cp(mid.at[:, part(ring(st, NB), B)], dgu.at[:, part(t, B)], s_mid.at[t])

        def write_dd(i, h, t):
            return cp(ddst.at[t], dd_ref.at[n, part(i, ROWS), :, part(h, HALF)], s_dd.at[t])

        def load_wd(j):
            return cp(wd_ref.at[layer, part(j, B)], wdj, s_wd)

        def load_wgu(j):
            return [cp(w.at[layer, :, part(j, B)], wgu.at[:, part(i, B)], s_wgu.at[i]) for i, w in enumerate((wg_ref, wu_ref))]

        def load_ps(k):
            t, at = ring(k, ES), (part(ring(k, E), EC), part(k // E, B))
            return cp(p.at[at], pa.at[t], s_ps.at[t, 0]), cp(s.at[at], sa.at[t], s_ps.at[t, 1])

        load_mid(0).start()
        load_wd(0).start()
        for k in range(ES - 1):
            start(load_ps(k))
        if n == 0:
            load_dh.wait()

        def tile(t, st, h):
            ddst[t] = tn(dgu[:, part(ring(st, 2), B)], dh[:, part(h, HALF)]).astype(bf16).reshape(ROWS, 8, HALF)

        def load_next(st, last):
            @when(st < last)
            def _():
                load_mid(st + 1).start()

            load_mid(st).wait()

        def down_by_half(st):
            load_next(st, 2 * NB - 1)
            t, i, h = ring(st, 2), ring(st, NB), st // NB
            tile(t, st, h)

            @when((st != 0) & (st != NB))
            def _():
                write_dd(ring(st - 1, NB), h, 1 - t).wait()

            write_dd(i, h, t).start()

            @when(i == NB - 1)
            def _():
                write_dd(i, h, t).wait()

            @when((st == 4) | (st == 6) | (st == 9))
            def _():
                dr.tick((st - 4) // 2, d_first, DP)

        def down(i):
            load_next(i, NB - 1)

            def each(h):
                @when(i > 0)
                def _():
                    write_dd(i - 1, h, h).wait()

                tile(h, i, h)
                write_dd(i, h, h).start()

            loop(2, each)
            gr.tick(GP + i, 0, GP)

        if n == 0:
            loop(2 * NB, down_by_half)
            load_a.wait()
        else:
            loop(NB, down)
            finish([write_dd(NB - 1, h, h) for h in range(2)])
            dr.tick(0, d_first, DP)
            load_a0.wait()
        ahead = 1 if n else 3

        def block(j):
            if n == 0:
                start(load_wgu(j))
            load_wd(j).wait()

            def act(i):
                k = j * E + i

                @when(k + ES - 1 < NB * E)
                def _():
                    start(load_ps(k + ES - 1))

                finish(load_ps(k))
                t, rows = ring(k, ES), part(i, EC)
                dm = dgu[rows, :B].astype(f32)
                dgu[rows, :B] = (dm * pa[t]).astype(bf16)
                dgu[rows, B:] = (dm * sa[t]).astype(bf16)

            def dmids(i):
                rows = part(i, R)
                dgu[rows, :B] = nt(dh[rows, :], wdj[...]).astype(bf16)
                loop(R // EC, lambda e: act(i * (R // EC) + e))

            loop(CHUNKS, dmids)

            @when(j + 1 < NB)
            def _():
                load_wd(j + 1).start()

            dr.tick(ahead + 2 * j, d_first, DP)

            @when(j >= 1)
            def _():
                gr.tick(2 * j - 1, g_first, GP)

            def terms(i):
                dwst[ring(n * NB + j, 2), part(i, 4)] = tn(a[:, part(i, R)], dgu[...]).astype(bf16).reshape(4, 2, 64, 2 * B)

            loop(D // R, terms)

            dr.tick(ahead + 1 + 2 * j, d_first, DP)
            gr.tick(2 * j, g_first, GP)

            if n == 0:
                finish(load_wgu(j))

                def back(i):
                    rows = part(i, R)
                    da[rows, :] += nt(dgu[rows, :], wgu[...])

                loop(CHUNKS, back)

        loop(NB, block)
        gr.tick(GP - 1, g_first, GP)
        if n == 0:
            load_h.start()
            load_h.wait()

            def norm(i):
                rows = part(i, N)
                wide = a[rows, :].astype(f32)
                d = da[rows, :].astype(bf16).astype(f32)
                scale = lax.rsqrt(jnp.mean(wide * wide, -1, keepdims=True) + 1e-6)
                inner = jnp.mean(d * wide, -1, keepdims=True)
                dn = (scale * d - wide * (scale * scale * scale * inner)).astype(bf16)
                dh[rows, :] = (dh[rows, :].astype(f32) + dn.astype(f32)).astype(bf16)

            loop(T // N, norm)
            load_a0.start()

    loop(NB, lambda t: gr.tick(GP + t, GP, GP))
    dr.close()
    gr.close()

    tot[0] = sums[...]
    for i, dev in enumerate((gr.partner, gr.across)):
        copy = remote(tot.at[i], got.at[i], s_tot.at[i], s_tot_in.at[i], dev)
        copy.start()
        copy.wait()
        tot[i + 1] = tot[i] + got[i]
    copies = [remote(tot.at[2], got.at[2 + z], s_tot.at[2 + i], s_tot_in.at[4 - i], dev) for i, dev in enumerate(gr.along)]
    start(copies)
    finish(copies)
    got[2 + z] = tot[2]
    sums_out[...] = got[2] + got[3] + got[4] + got[5]


def backward(*arrays):
    return pl.pallas_call(
        backward_kernel,
        out_shape=(
            jax.ShapeDtypeStruct((2, 2, 64, FF), bf16),
            jax.ShapeDtypeStruct((2, 25, 8, D), bf16),
            jax.ShapeDtypeStruct((8, 128), f32),
            jax.ShapeDtypeStruct((2, FF // 8, 8, D), bf16),
        ),
        in_specs=[pl.BlockSpec(memory_space=HBM)] * len(arrays),
        out_specs=tuple(pl.BlockSpec(memory_space=m) for m in (HBM, HBM, VMEM, HBM)),
        scratch_shapes=[
            VMEM((8, 128), f32), VMEM((T, D), bf16), VMEM((T, D), bf16), VMEM((T, D), f32), VMEM((ES, EC, B), f32), VMEM((ES, EC, B), f32),
            VMEM((T, 2 * B), bf16), VMEM((D, 2 * B), bf16), VMEM((B, D), bf16), VMEM((2, 8, 2, 64, 2 * B), bf16),
            VMEM((2, ROWS, 8, HALF), bf16), VMEM((DS[0], 8, 25, 8, DC), bf16),
            VMEM((3, 8, 128), f32), VMEM((6, 8, 128), f32), DMA((5,)), DMA((5,)),
            DMA, DMA, DMA((ES, 2)), DMA((2,)), DMA((2,)), DMA, DMA((2,)), DMA((DS[0], 8)),
        ] + Reducer.scratch((64, B), 1, GS) + Reducer.scratch((25, 8, DC), 8, DS),
        compiler_params=pltpu.CompilerParams(collective_id=0, has_side_effects=True, vmem_limit_bytes=67043328),
    )(*arrays)


def gather_kernel(sg, su, sd, og, ou, od, zss, zrs, yss, yrs, dss, drs, ls):
    r, y, z, c = place()
    greet(r, y, z, c)
    chunks = [(s, o, layer) for layer in range(2) for s, o in ((sg, og), (su, ou), (sd, od))]
    last = len(chunks) - 1
    entries = [(k, y) for k in range(last + 1)] + [(last, 1 - y)]
    partner, across = device(r, y, z, 1 - c), device(r, 1 - y, z, c)
    beside = device(r, y, ring(z + 1, 4), c), device(r, y, ring(z + 3, 4), c)
    sides = range(2)
    goes_on = z < 3, z > 0

    def there(d, side):
        return z + d <= 3 if side else z >= d

    def at(d, side):
        return z + d if side else z - d

    def block(k, row, zz, c=c):
        return chunks[k][1].at[chunks[k][2], row * 8 + zz * 2 + c]

    def along(src, e, zz, d, side):
        k, row = entries[e]
        when(goes_on[side])(remote(src, block(k, row, zz), zss.at[e, d - 1, side], zrs.at[e, d - 1, side], beside[side]).start)

    def over(src, k, zz, w):
        remote(src, block(k, y, zz), yss.at[k, w], yrs.at[k, w], across).start()

    def pair(src, k, row, zz):
        remote(src, block(k, row, zz), dss.at[k, row * 4 + zz], drs.at[k, row * 4 + zz], partner).start()

    def arrived(ref, sem):
        remote(ref, ref, sem, sem, partner).wait_recv()
        return ref

    def left(ref, sem):
        remote(ref, ref, sem, sem, partner).wait_send()

    def which(d, side):
        return 2 * d - 1 + side

    own = [s.at[layer] for s, _, layer in chunks]
    for k in [last, *range(last)]:
        over(own[k], k, z, 0)
    kept = [pltpu.make_async_copy(src, block(k, y, z), ls.at[k]) for k, src in enumerate(own)]
    for k, src in enumerate(own):
        for side in sides:
            along(src, k, z, 1, side)
        pair(src, k, y, z)
        kept[k].start()
    src = arrived(block(last, 1 - y, z), yrs.at[last, 0])
    for side in sides:
        along(src, last + 1, z, 1, side)
    pair(src, last, 1 - y, z)

    def crossed(d, k):
        for side in sides[: 1 + min(d, 1)]:

            def hand(zz, w):
                pair(arrived(block(k, 1 - y, zz), yrs.at[k, w]), k, 1 - y, zz)

            if d:
                when(there(d, side))(functools.partial(hand, at(d, side), which(d, side)))
            else:
                hand(z, 0)

    for d in (1, 2, 3):
        for e, (k, row) in enumerate(entries):
            for side in sides:

                @when(there(d, side))
                def _():
                    zz = at(d, side)
                    src = arrived(block(k, row, zz), zrs.at[e, d - 1, side])
                    if d < 3:
                        along(src, e, zz, d + 1, side)
                    if k != last:
                        over(src, k, zz, which(d, side))
                    pair(src, k, row, zz)

            if k != last:
                crossed(d - 1, k)
    for k in range(last):
        crossed(3, k)

    for k in range(last + 1):
        for b in range(8):
            left(arrived(block(k, 0, b, 1 - c), drs.at[k, b]), dss.at[k, b])
        left(own[k], yss.at[k, 0])
    for d in range(3):
        for side in sides:
            for e in range(len(entries)):
                when(goes_on[side] & there(d, side))(functools.partial(left, own[entries[e][0]], zss.at[e, d, side]))
            for k in range(last):
                when(there(d + 1, side))(functools.partial(left, own[k], yss.at[k, which(d + 1, side)]))
    finish(kept)


def all_gather(*shards):
    out = pl.pallas_call(
        gather_kernel,
        out_shape=[jax.ShapeDtypeStruct((2, 16, *s.shape[1:]), bf16) for s in shards],
        in_specs=[pl.BlockSpec(memory_space=HBM)] * 3,
        out_specs=[pl.BlockSpec(memory_space=pl.ANY)] * 3,
        scratch_shapes=[DMA((7, 3, 2)), DMA((7, 3, 2)), DMA((6, 7)), DMA((6, 7)), DMA((6, 8)), DMA((6, 8)), DMA((6,))],
        compiler_params=pltpu.CompilerParams(collective_id=1, has_side_effects=True, vmem_limit_bytes=2**23),
    )(*shards)
    return [o.reshape(2, -1, o.shape[-1]) for o in out]


def adamw(w, m, v, g):
    m = 0.9 * m + 0.1 * g
    v = 0.95 * v + 0.05 * g * g
    step = m * lax.rsqrt(v + 1e-8) + 0.1 * w
    return (w - 0.02 * step).astype(bf16), m, v


def solution(mesh):
    def step(x, dy, wg, wu, wd, mg, mu, md, vg, vu, vd):
        a0, a1, h1, p0, s0, mid0, p1, s1, mid1 = forward(x[0], wg, wu, wd)
        gg, gd, sums, _ = backward(dy[0], h1, a1, a0, p1, s1, mid1, p0, s0, mid0, wg, wu, wd)
        factor = jnp.minimum(1.0, 0.5 * lax.rsqrt(jnp.sum(sums) / (6 * D * FF) + 1e-30))
        me = lax.axis_index("dp")
        new = []
        for w, m, v, g in ((wg, mg, vg, gg[0]), (wu, mu, vu, gg[1]), (wd, md, vd, gd.reshape(2, 200, D))):
            rows = m.shape[1]
            mine = lax.dynamic_slice_in_dim(w, me * rows, rows, 1)
            new.append(adamw(mine.astype(f32), m, v, g.astype(f32) * factor))
        weights = all_gather(*(n[0] for n in new))
        return (*weights, *(n[1] for n in new), *(n[2] for n in new))

    seq, rep, own = P(("rep", "dp")), P("rep"), P("rep", "dp")
    return jax.shard_map(
        step,
        mesh=mesh,
        in_specs=(seq, seq, P(), P(), P(), *[P(None, "dp")] * 6),
        out_specs=(rep,) * 3 + (own,) * 6,
        check_vma=False,
    )
```

time: 1890 us -> 624 us (0.33)
  waiting for transfers between devices: 824 us -> 0 us
  Pallas kernels: 0 us -> 595 us
  matrix products: 461 us -> 0 us
  starting transfers between devices: 231 us -> 0 us
  other arithmetic: 156 us -> 12.8 us
  local copies, waits for them, and re-layouts: 105 us -> 14.8 us
  loops' own time: 49.3 us -> 0 us
  blocking collectives: 30.6 us -> 0 us
    pallas_call x0 -> x3, Pallas kernels: none -> 595 us  [the longest x1 299 us: backward(): pl.pallas_call(backward_kernel, out_shape=(jax.ShapeDtypeStruct((2, 2, 64...]
    dot_general x102 -> x0, waiting for transfers between devices: 514 us -> none  [the longest x34 186 us: layer(): up = jnp.dot(a, w['w_up'], preferred_element_type=jnp.float32)]
    dot_general x57 -> x0, matrix products: 461 us -> none  [the longest x19 171 us: matmul(): jnp.dot(a, w, preferred_element_type=jnp.float32).astype(jnp.bfloat16)]
    reshape x3 -> x0, waiting for transfers between devices: 309 us -> none  [step(): t.reshape(-1, *t.shape[2:])]
    dot_general x102 -> x0, starting transfers between devices: 231 us -> none  [the longest x34 81 us: layer(): gate = jnp.dot(a, w['w_gate'], preferred_element_type=jnp.float32)]
    dot_general x112 -> x0, other arithmetic: 112 us -> none
    unnamed x63 -> x3, local copies, waits for them, and re-layouts: 88.9 us -> 14.8 us
    another operation x6 -> x0, loops' own time: 49.3 us -> none  [the longest x2 16.6 us: layer(): gate = jnp.dot(a, w['w_gate'], preferred_element_type=jnp.float32)]
  transfers between devices with their start and end apart: 105 -> 0, of which waited for: 60 -> 0; matrix products, arithmetic and copies ran while one was open for 21% -> 0% of each run, Pallas kernels for 0% -> 0%
where the time goes in v3:
time: 624 us
  Pallas kernels  595 us (95%)
  local copies, waits for them, and re-layouts  14.8 us (2%)
  other arithmetic  12.8 us (2%)
    pallas_call x1, Pallas kernels, backward(): pl.pallas_call(backward_kernel, out_shape=(jax.ShapeDtypeStruct((2, 2, 64...  299 us
    pallas_call x1, Pallas kernels, all_gather(): pl.pallas_call(gather_kernel, out_shape=[jax.ShapeDtypeStruct((2, 16, *s....  193 us
    pallas_call x1, Pallas kernels, forward(): pl.pallas_call(forward_kernel, out_shape=(states,) * 3 + (wide, wide, mid...  103 us
    unnamed x3, local copies, waits for them, and re-layouts  14.8 us

profile of v3, /device:TPU:0, one launch (start us, length us, event | category | flops | bytes accessed | tf_op | source)
XLA Modules:
  0.0 623.6 jit_solution(18073704533102196993)
XLA Ops:
  0.6 102.8 %shard_map.178 = (bf16[2048,1024]{1,0:T(8,128)(2,1)}, bf16[2048,1024]{1,0:T(8,128)(2,1)}, bf16[2048,1024]{1,0:T(8,128)(2,1)}, f32[2048,3200]{1,0:T(8,128)}, f32[...) custom-call(bf16[2048,1024]{1,0:T(8,128)(2,1)} %bitcast.30, ...), custom_call_target="tpu_custom_call" | custom-call | tf_op jit(solution)/shard_map/pallas_call | solution.py:195
  103.4 298.6 %shard_map.179 = (bf16[2,2,64,3200]{3,2,1,0:T(8,128)(2,1)}, bf16[2,25,8,1024]{3,2,1,0:T(8,128)(2,1)}, f32[8,128]{1,0:T(8,128)}, bf16[2,400,8,1024]{3,2,1,0:T(8,128)(2,1)}) custom-call(bf16[2048,1024]{1,0:T(8,128)(2,1)} %bitcast.29, bf16[2048,1024]{1,0:T(8,128)(2,1)} %get-tuple-element.24.h1_ref, bf16[2048,1024]{1,0:T(8,128)(2,1)} %get-tuple-element.25.a1_ref, ...), custom_call_target="tpu_custom_call" | custom-call | tf_op jit(solution)/shard_map/pallas_call | solution.py:586
  402.0 1.3 reduce_sum.9
  404.0 5.1 fusion.8
  409.1 6.4 %fusion.5 = (bf16[2,64,3200]{2,1,0:T(8,128)(2,1)S(1)}, f32[2,64,3200]{2,1,0:T(8,128)}, f32[2,64,3200]{2,1,0:T(8,128)}, bf16[2,64,3200]{2,1,0:T(8,128)(2,1)S(1)},...) fusion(bf16[2,1024,3200]{2,1,0:T(8,128)(2,1)} %wu_ref.3, s32[]{:T(128)S(6)} %select_n.7, f32[]{:T(128)S(6)} %min_shard_map.3, ...), kind=kLoop, calls=%fused_computation.14 | loop fusion | flops 13926400 | bytes 18022408 | tf_op jit(solution)/shard_map/convert_element_type | solution.py:720
  415.6 193.2 %shard_map.180 = (bf16[2,16,64,3200]{3,2,1,0:T(8,128)(2,1)S(1)}, bf16[2,16,64,3200]{3,2,1,0:T(8,128)(2,1)S(1)}, bf16[2,16,200,1024]{3,2,1,0:T(8,128)(2,1)S(1)}) custom-call(bf16[2,64,3200]{2,1,0:T(8,128)(2,1)S(1)} %get-tuple-element.48.sg, bf16[2,64,3200]{2,1,0:T(8,128)(2,1)S(1)} %get-tuple-element.42.su, bf16[2,200,1024]{2,1,0:T(8,128)(2,1)S(1)} %get-tuple-element.39.sd), custom_call_target="tpu_custom_call" | custom-call | tf_op jit(solution)/shard_map/pallas_call | solution.py:705
  608.8 5.0 copy.23
  613.7 4.9 copy.24
  618.7 4.9 copy.25

commit v4 on v3

--- a/solution.py
+++ b/solution.py
@@ -88,7 +88,7 @@
 def forward_kernel(
     x_ref, wg_ref, wu_ref, wd_ref,
     a0_ref, a1_ref, h1_ref, p0, s0, m0, p1, s1, m1,
-    x, a, total, wgu, wdj, g, stp, sts, sta, stb, s_x, s_out, s_wg, s_wu, s_wd, s_p, s_s, s_m,
+    x, a, mid, wgu, wd, g, stp, sts, s_x, s_out, s_wg, s_wu, s_wd, s_p, s_s, s_m,
 ):
     cp = pltpu.make_async_copy
 
@@ -97,16 +97,10 @@
         return (cp(wg_ref.at[n // NB, :, cols], wgu.at[s, :, pl.ds(0, B)], s_wg.at[s]),
                 cp(wu_ref.at[n // NB, :, cols], wgu.at[s, :, pl.ds(B, B)], s_wu.at[s]))
 
-    def load_wd(j):
-        s = ring(j, 2)
-        return cp(wd_ref.at[0, part(j, B)], wdj.at[s], s_wd.at[s])
-
-    load_x = cp(x_ref, x, s_x)
+    load_x, load_wd = cp(x_ref, x, s_x), cp(wd_ref.at[0], wd, s_wd)
     load_x.start()
     start(load_w(0))
-    total[...] = jnp.zeros_like(total)
-    stb[...] = jnp.zeros_like(stb)
-    load_wd(0).start()
+    load_wd.start()
     load_x.wait()
 
     def norm(i):
@@ -116,20 +110,16 @@
     loop(T // N, norm)
     out_a0 = cp(a, a0_ref, s_out.at[0])
     out_a0.start()
-    load_wd(0).wait()
     for layer, (p, s, m) in enumerate(((p0, s0, m0), (p1, s1, m1))):
 
-        def writes(k, even):
-            t, u, at = ring(k, FS), ring(k // 2, FS // 2), (part(ring(k, CHUNKS), R), part(k // CHUNKS, B))
-            return cp(stp.at[t], p.at[at], s_p.at[t]), cp(sts.at[t], s.at[at], s_s.at[t]), cp((sta if even else stb).at[u], m.at[at], s_m.at[t])
-
-        def down(k, even):
-            mid = (sta if even else stb)[ring(k // 2, FS // 2)]
-            total[part(ring(k, CHUNKS), R), :] += nn(mid, wdj[ring(k // CHUNKS, 2)])
-
-        def step(k, even):
+        def writes(k):
+            t, at = ring(k, FS), (part(ring(k, CHUNKS), R), part(k // CHUNKS, B))
+            return cp(stp.at[t], p.at[at], s_p.at[t]), cp(sts.at[t], s.at[at], s_s.at[t]), cp(mid.at[at], m.at[at], s_m.at[t])
+
+        def step(k):
             j, i, t = k // CHUNKS, ring(k, CHUNKS), ring(k, FS)
             n = layer * NB + j
+            rows = part(i, R)
 
             @when(i == 0)
             def _():
@@ -139,53 +129,35 @@
                 def _():
                     start(load_w(n + 1))
 
-            if layer == 0:
-
-                @when(i == 1)
-                def _():
-                    @when(j > 0)
-                    def _():
-                        load_wd(j).wait()
-
-                    @when(j + 1 < NB)
-                    def _():
-                        load_wd(j + 1).start()
-
             @when(k >= FS)
             def _():
-                finish(writes(k - FS, even))
-
-            g[...] = nn(a[part(i, R), :], wgu[ring(n, 2)])
-            if layer == 0:
-                down(jnp.where(k == 0, STEPS - 1, k - 1), not even)
+                finish(writes(k - FS))
+
+            g[...] = nn(a[rows, :], wgu[ring(n, 2)])
             gate, up = g[:, :B], g[:, B:]
             sig = 0.5 + 0.5 * jnp.tanh(0.5 * gate)
             silu = gate * sig
-            (sta if even else stb)[ring(k // 2, FS // 2)] = (silu * up).astype(bf16)
+            mid[rows, part(j, B)] = (silu * up).astype(bf16)
             stp[t] = up * (sig + silu * (1.0 - sig))
             sts[t] = silu
-            start(writes(k, even))
-
-        def steps(i):
-            step(2 * i, True)
-            step(2 * i + 1, False)
-
-        loop(STEPS // 2, steps)
+            start(writes(k))
+
+        loop(STEPS, step)
         if layer == 0:
-            down(STEPS - 1, False)
-        for k in range(STEPS - FS, STEPS):
-            finish(writes(k, k % 2 == 0))
-        if layer == 0:
+            load_wd.wait()
             out_a0.wait()
-            def joint(i):
-                rows = part(i, N)
-                h = (x[rows, :].astype(f32) + total[rows, :].astype(bf16).astype(f32)).astype(bf16)
+
+            def down(i):
+                rows = part(i, R)
+                h = (x[rows, :].astype(f32) + nn(mid[rows, :], wd[...]).astype(bf16).astype(f32)).astype(bf16)
                 x[rows, :] = h
                 a[rows, :] = normed(h)
 
-            loop(T // N, joint)
+            loop(CHUNKS, down)
             outs = cp(x, h1_ref, s_out.at[0]), cp(a, a1_ref, s_out.at[1])
             start(outs)
+        for k in range(STEPS - FS, STEPS):
+            finish(writes(k))
     finish(outs)
 
 
@@ -198,9 +170,9 @@
         in_specs=[pl.BlockSpec(memory_space=HBM)] * 4,
         out_specs=(pl.BlockSpec(memory_space=HBM),) * 9,
         scratch_shapes=[
-            VMEM((T, D), bf16), VMEM((T, D), bf16), VMEM((T, D), f32), VMEM((2, D, 2 * B), bf16), VMEM((2, B, D), bf16),
-            VMEM((R, 2 * B), f32), VMEM((FS, R, B), f32), VMEM((FS, R, B), f32), VMEM((FS // 2, R, B), bf16), VMEM((FS // 2, R, B), bf16),
-            DMA, DMA(two), DMA(two), DMA(two), DMA(two), DMA((FS,)), DMA((FS,)), DMA((FS,)),
+            VMEM((T, D), bf16), VMEM((T, D), bf16), VMEM((T, FF), bf16), VMEM((2, D, 2 * B), bf16), VMEM((FF, D), bf16),
+            VMEM((R, 2 * B), f32), VMEM((FS, R, B), f32), VMEM((FS, R, B), f32),
+            DMA, DMA(two), DMA(two), DMA(two), DMA, DMA((FS,)), DMA((FS,)), DMA((FS,)),
         ],
         compiler_params=pltpu.CompilerParams(vmem_limit_bytes=67043328),
     )(x, wg, wu, wd)
@@ -324,8 +296,8 @@
         self.copy_out(q).start()
 
     def tick(self, t, first, count):
-        for lag, stage in zip(self.LAGS[::-1], (self.stage3, self.stage2, self.stage1, self.stage0), strict=True):
-            q = t - lag
+        for i, stage in ((1, self.stage1), (0, self.stage0), (2, self.stage2), (3, self.stage3)):
+            q = t - self.LAGS[i]
             when((q >= 0) & (q < count))(functools.partial(stage, first + q))
 
     def close(self):
@@ -366,9 +338,9 @@
 DC, DP = 256, 4
 GP = 2 * NB
 HALF = 512
-GS, DS = (2, 3, 3), (2, 2, 2)
-EC, ES = 256, 6
-E = T // EC
+GS, DS = (2, 3, 3), (2, 3, 3)
+MS = 3
+ES = 3
 ROWS = B // 8
 
 
@@ -386,7 +358,6 @@
     load_a = cp(a1_ref, a, s_a)
     load_h, load_a0 = cp(h1_ref, a, s_a), cp(a0_ref, a, s_a)
     load_dh.start()
-    load_a.start()
     greet(r, y, z, c)
     sums[...] = jnp.zeros_like(sums)
     da[...] = jnp.zeros_like(da)
@@ -419,7 +390,7 @@
         layer, d_first, g_first = 1 - n, n * DP, n * GP
 
         def load_mid(st):
-            t = ring(st, 2)
+            t = ring(st, MS)
             return cp(mid.at[:, part(ring(st, NB), B)], dgu.at[:, part(t, B)], s_mid.at[t])
 
         def write_dd(i, h, t):
@@ -432,126 +403,19 @@
             return [cp(w.at[layer, :, part(j, B)], wgu.at[:, part(i, B)], s_wgu.at[i]) for i, w in enumerate((wg_ref, wu_ref))]
 
         def load_ps(k):
-            t, at = ring(k, ES), (part(ring(k, E), EC), part(k // E, B))
+            t, at = ring(k, ES), (part(ring(k, CHUNKS), R), part(k // CHUNKS, B))
             return cp(p.at[at], pa.at[t], s_ps.at[t, 0]), cp(s.at[at], sa.at[t], s_ps.at[t, 1])
 
-        load_mid(0).start()
-        load_wd(0).start()
-        for k in range(ES - 1):
-            start(load_ps(k))
+        def first_loads():
+            load_wd(0).start()
+            for k in range(ES - 1):
+                start(load_ps(k))
+
+        for k in range(MS - 1):
+            load_mid(k).start()
         if n == 0:
             load_dh.wait()
-
-        def tile(t, st, h):
-            ddst[t] = tn(dgu[:, part(ring(st, 2), B)], dh[:, part(h, HALF)]).astype(bf16).reshape(ROWS, 8, HALF)
-
-        def load_next(st, last):
-            @when(st < last)
-            def _():
-                load_mid(st + 1).start()
-
-            load_mid(st).wait()
-
-        def down_by_half(st):
-            load_next(st, 2 * NB - 1)
-            t, i, h = ring(st, 2), ring(st, NB), st // NB
-            tile(t, st, h)
-
-            @when((st != 0) & (st != NB))
-            def _():
-                write_dd(ring(st - 1, NB), h, 1 - t).wait()
-
-            write_dd(i, h, t).start()
-
-            @when(i == NB - 1)
-            def _():
-                write_dd(i, h, t).wait()
-
-            @when((st == 4) | (st == 6) | (st == 9))
-            def _():
-                dr.tick((st - 4) // 2, d_first, DP)
-
-        def down(i):
-            load_next(i, NB - 1)
-
-            def each(h):
-                @when(i > 0)
-                def _():
-                    write_dd(i - 1, h, h).wait()
-
-                tile(h, i, h)
-                write_dd(i, h, h).start()
-
-            loop(2, each)
-            gr.tick(GP + i, 0, GP)
-
-        if n == 0:
-            loop(2 * NB, down_by_half)
-            load_a.wait()
         else:
-            loop(NB, down)
-            finish([write_dd(NB - 1, h, h) for h in range(2)])
-            dr.tick(0, d_first, DP)
-            load_a0.wait()
-        ahead = 1 if n else 3
-
-        def block(j):
-            if n == 0:
-                start(load_wgu(j))
-            load_wd(j).wait()
-
-            def act(i):
-                k = j * E + i
-
-                @when(k + ES - 1 < NB * E)
-                def _():
-                    start(load_ps(k + ES - 1))
-
-                finish(load_ps(k))
-                t, rows = ring(k, ES), part(i, EC)
-                dm = dgu[rows, :B].astype(f32)
-                dgu[rows, :B] = (dm * pa[t]).astype(bf16)
-                dgu[rows, B:] = (dm * sa[t]).astype(bf16)
-
-            def dmids(i):
-                rows = part(i, R)
-                dgu[rows, :B] = nt(dh[rows, :], wdj[...]).astype(bf16)
-                loop(R // EC, lambda e: act(i * (R // EC) + e))
-
-            loop(CHUNKS, dmids)
-
-            @when(j + 1 < NB)
-            def _():
-                load_wd(j + 1).start()
-
-            dr.tick(ahead + 2 * j, d_first, DP)
-
-            @when(j >= 1)
-            def _():
-                gr.tick(2 * j - 1, g_first, GP)
-
-            def terms(i):
-                dwst[ring(n * NB + j, 2), part(i, 4)] = tn(a[:, part(i, R)], dgu[...]).astype(bf16).reshape(4, 2, 64, 2 * B)
-
-            loop(D // R, terms)
-
-            dr.tick(ahead + 1 + 2 * j, d_first, DP)
-            gr.tick(2 * j, g_first, GP)
-
-            if n == 0:
-                finish(load_wgu(j))
-
-                def back(i):
-                    rows = part(i, R)
-                    da[rows, :] += nt(dgu[rows, :], wgu[...])
-
-                loop(CHUNKS, back)
-
-        loop(NB, block)
-        gr.tick(GP - 1, g_first, GP)
-        if n == 0:
-            load_h.start()
-            load_h.wait()
 
             def norm(i):
                 rows = part(i, N)
@@ -562,9 +426,103 @@
                 dn = (scale * d - wide * (scale * scale * scale * inner)).astype(bf16)
                 dh[rows, :] = (dh[rows, :].astype(f32) + dn.astype(f32)).astype(bf16)
 
+            load_h.wait()
             loop(T // N, norm)
-            load_a0.start()
-
+
+        def tile(t, st, h):
+            ddst[t] = tn(dgu[:, part(ring(st, MS), B)], dh[:, part(h, HALF)]).astype(bf16).reshape(ROWS, 8, HALF)
+
+        def down(st):
+            @when(st + MS - 1 < 2 * NB)
+            def _():
+                load_mid(st + MS - 1).start()
+
+            @when(st == 1)
+            def _():
+                (load_a0 if n else load_a).start()
+                first_loads()
+
+            load_mid(st).wait()
+            t, i, h = ring(st, 2), ring(st, NB), st // NB
+            tile(t, st, h)
+
+            @when((st != 0) & (st != NB))
+            def _():
+                write_dd(ring(st - 1, NB), h, 1 - t).wait()
+
+            write_dd(i, h, t).start()
+
+            @when(i == NB - 1)
+            def _():
+                write_dd(i, h, t).wait()
+
+            @when((st == 4) | (st == 6) | (st == 9))
+            def _():
+                dr.tick((st - 4) // 2, d_first, DP)
+
+            if n:
+
+                @when((st == 0) | (st == 2) | (st == 5) | (st == 7) | (st == 9))
+                def _():
+                    gr.tick(GP + st // 2, 0, GP)
+
+        loop(2 * NB, down)
+        (load_a0 if n else load_a).wait()
+
+        def block(j):
+            if n == 0:
+                start(load_wgu(j))
+            load_wd(j).wait()
+
+            def dmids(i):
+                k, rows = j * CHUNKS + i, part(i, R)
+                t = ring(k, ES)
+
+                @when(k + ES - 1 < NB * CHUNKS)
+                def _():
+                    start(load_ps(k + ES - 1))
+
+                finish(load_ps(k))
+                dm = nt(dh[rows, :], wdj[...]).astype(bf16).astype(f32)
+                dgu[rows, :B] = (dm * pa[t]).astype(bf16)
+                dgu[rows, B : 2 * B] = (dm * sa[t]).astype(bf16)
+
+            loop(CHUNKS, dmids)
+
+            @when(j + 1 < NB)
+            def _():
+                load_wd(j + 1).start()
+
+            dr.tick(3 + 2 * j, d_first, DP)
+
+            @when(j >= 1)
+            def _():
+                gr.tick(2 * j - 1, g_first, GP)
+
+            def terms(i):
+                dwst[ring(n * NB + j, 2), part(i, 4)] = tn(a[:, part(i, R)], dgu[:, : 2 * B]).astype(bf16).reshape(4, 2, 64, 2 * B)
+
+            loop(D // R, terms)
+
+            dr.tick(4 + 2 * j, d_first, DP)
+            gr.tick(2 * j, g_first, GP)
+
+            if n == 0:
+
+                @when(j == NB - 1)
+                def _():
+                    load_h.start()
+
+                finish(load_wgu(j))
+
+                def back(i):
+                    rows = part(i, R)
+                    da[rows, :] += nt(dgu[rows, : 2 * B], wgu[...])
+
+                loop(CHUNKS, back)
+
+        loop(NB, block)
+        gr.tick(GP - 1, g_first, GP)
     loop(NB, lambda t: gr.tick(GP + t, GP, GP))
     dr.close()
     gr.close()
@@ -594,11 +552,11 @@
         in_specs=[pl.BlockSpec(memory_space=HBM)] * len(arrays),
         out_specs=tuple(pl.BlockSpec(memory_space=m) for m in (HBM, HBM, VMEM, HBM)),
         scratch_shapes=[
-            VMEM((8, 128), f32), VMEM((T, D), bf16), VMEM((T, D), bf16), VMEM((T, D), f32), VMEM((ES, EC, B), f32), VMEM((ES, EC, B), f32),
-            VMEM((T, 2 * B), bf16), VMEM((D, 2 * B), bf16), VMEM((B, D), bf16), VMEM((2, 8, 2, 64, 2 * B), bf16),
+            VMEM((8, 128), f32), VMEM((T, D), bf16), VMEM((T, D), bf16), VMEM((T, D), f32), VMEM((ES, R, B), f32), VMEM((ES, R, B), f32),
+            VMEM((T, MS * B), bf16), VMEM((D, 2 * B), bf16), VMEM((B, D), bf16), VMEM((2, 8, 2, 64, 2 * B), bf16),
             VMEM((2, ROWS, 8, HALF), bf16), VMEM((DS[0], 8, 25, 8, DC), bf16),
             VMEM((3, 8, 128), f32), VMEM((6, 8, 128), f32), DMA((5,)), DMA((5,)),
-            DMA, DMA, DMA((ES, 2)), DMA((2,)), DMA((2,)), DMA, DMA((2,)), DMA((DS[0], 8)),
+            DMA, DMA, DMA((ES, 2)), DMA((MS,)), DMA((2,)), DMA, DMA((2,)), DMA((DS[0], 8)),
         ] + Reducer.scratch((64, B), 1, GS) + Reducer.scratch((25, 8, DC), 8, DS),
         compiler_params=pltpu.CompilerParams(collective_id=0, has_side_effects=True, vmem_limit_bytes=67043328),
     )(*arrays)

time: 624 us -> 585 us (0.938)
  Pallas kernels: 595 us -> 555 us
    pallas_call x1, Pallas kernels: 299 us -> 272 us  [backward(): pl.pallas_call(backward_kernel, out_shape=(jax.ShapeDtypeStruct((2, 2, 64...]
    pallas_call x1, Pallas kernels: 103 us -> 89.8 us  [forward(): pl.pallas_call(forward_kernel, out_shape=(states,) * 3 + (wide, wide, mid...]
where the time goes in v4:
time: 585 us; the launch traced here: 584 us
  Pallas kernels  555 us (95%)
  local copies, waits for them, and re-layouts  14.8 us (3%)
  other arithmetic  12.8 us (2%)
    pallas_call x1, Pallas kernels, backward(): pl.pallas_call(backward_kernel, out_shape=(jax.ShapeDtypeStruct((2, 2, 64...  272 us
    pallas_call x1, Pallas kernels, all_gather(): pl.pallas_call(gather_kernel, out_shape=[jax.ShapeDtypeStruct((2, 16, *s....  193 us
    pallas_call x1, Pallas kernels, forward(): pl.pallas_call(forward_kernel, out_shape=(states,) * 3 + (wide, wide, mid...  89.8 us
    unnamed x3, local copies, waits for them, and re-layouts  14.8 us

profile of v4, /device:TPU:0, one launch (start us, length us, event | category | flops | bytes accessed | tf_op | source)
XLA Modules:
  0.0 584.4 jit_solution(5917441212293277412)
XLA Ops:
  0.6 89.8 %shard_map.178 = (bf16[2048,1024]{1,0:T(8,128)(2,1)}, bf16[2048,1024]{1,0:T(8,128)(2,1)}, bf16[2048,1024]{1,0:T(8,128)(2,1)}, f32[2048,3200]{1,0:T(8,128)}, f32[...) custom-call(bf16[2048,1024]{1,0:T(8,128)(2,1)} %bitcast.30, ...), custom_call_target="tpu_custom_call" | custom-call | tf_op jit(solution)/shard_map/pallas_call | solution.py:167
  90.4 272.4 %shard_map.179 = (bf16[2,2,64,3200]{3,2,1,0:T(8,128)(2,1)}, bf16[2,25,8,1024]{3,2,1,0:T(8,128)(2,1)}, f32[8,128]{1,0:T(8,128)}, bf16[2,400,8,1024]{3,2,1,0:T(8,128)(2,1)}) custom-call(bf16[2048,1024]{1,0:T(8,128)(2,1)} %bitcast.29, bf16[2048,1024]{1,0:T(8,128)(2,1)} %get-tuple-element.24.h1_ref, bf16[2048,1024]{1,0:T(8,128)(2,1)} %get-tuple-element.25.a1_ref, ...), custom_call_target="tpu_custom_call" | custom-call | tf_op jit(solution)/shard_map/pallas_call | solution.py:544
  362.8 1.3 reduce_sum.9
  364.8 5.1 fusion.8
  370.0 6.4 %fusion.5 = (bf16[2,64,3200]{2,1,0:T(8,128)(2,1)S(1)}, f32[2,64,3200]{2,1,0:T(8,128)}, f32[2,64,3200]{2,1,0:T(8,128)}, bf16[2,64,3200]{2,1,0:T(8,128)(2,1)S(1)},...) fusion(bf16[2,1024,3200]{2,1,0:T(8,128)(2,1)} %wu_ref.3, s32[]{:T(128)S(6)} %select_n.7, f32[]{:T(128)S(6)} %min_shard_map.3, ...), kind=kLoop, calls=%fused_computation.14 | loop fusion | flops 13926400 | bytes 18022408 | tf_op jit(solution)/shard_map/convert_element_type | solution.py:678
  376.4 193.2 %shard_map.180 = (bf16[2,16,64,3200]{3,2,1,0:T(8,128)(2,1)S(1)}, bf16[2,16,64,3200]{3,2,1,0:T(8,128)(2,1)S(1)}, bf16[2,16,200,1024]{3,2,1,0:T(8,128)(2,1)S(1)}) custom-call(bf16[2,64,3200]{2,1,0:T(8,128)(2,1)S(1)} %get-tuple-element.48.sg, bf16[2,64,3200]{2,1,0:T(8,128)(2,1)S(1)} %get-tuple-element.42.su, bf16[2,200,1024]{2,1,0:T(8,128)(2,1)S(1)} %get-tuple-element.39.sd), custom_call_target="tpu_custom_call" | custom-call | tf_op jit(solution)/shard_map/pallas_call | solution.py:663
  569.6 5.0 copy.23
  574.5 4.9 copy.24
  579.5 4.9 copy.25

commit v5 on v4

--- a/solution.py
+++ b/solution.py
@@ -27,9 +27,9 @@
     return (r, y * 8 + z * 2 + c)
 
 
-def greet(r, y, z, c):
+def greet(r, y, z, c, *more):
     bar = pltpu.get_barrier_semaphore()
-    peers = [device(r, y, z, 1 - c), device(r, 1 - y, z, c)] + [device(r, y, ring(z + o, 4), c) for o in (1, 2, 3)]
+    peers = [device(r, y, z, 1 - c), device(r, 1 - y, z, c)] + [device(r, y, ring(z + o, 4), c) for o in (1, 2, 3)] + list(more)
     for p in peers:
         signal(bar, p)
     pl.semaphore_wait(bar, len(peers))
@@ -300,6 +300,10 @@
             q = t - self.LAGS[i]
             when((q >= 0) & (q < count))(functools.partial(stage, first + q))
 
+    def run(self, stages, first):
+        for stage, q in stages:
+            (self.stage0, self.stage1, self.stage2, self.stage3)[stage](first + q)
+
     def close(self):
         finish([self.copy_out(self.total - self.nz + i) for i in range(self.nz)])
 
@@ -342,6 +346,13 @@
 MS = 3
 ES = 3
 ROWS = B // 8
+
+
+STAGES = (
+    ((4, ((0, 0), (0, 1))), (6, ((1, 0), (1, 1))), (9, ((0, 2), (0, 3), (2, 0)))),
+    ((0, ((1, 2), (1, 3), (2, 1))), (1, ((2, 3), (3, 1))), (2, ((3, 3),))),
+    ((0, ((2, 2), (3, 0))), (1, ((3, 2),))),
+)
 
 
 def backward_kernel(
@@ -358,9 +369,6 @@
     load_a = cp(a1_ref, a, s_a)
     load_h, load_a0 = cp(h1_ref, a, s_a), cp(a0_ref, a, s_a)
     load_dh.start()
-    greet(r, y, z, c)
-    sums[...] = jnp.zeros_like(sums)
-    da[...] = jnp.zeros_like(da)
 
     def g_part(q):
         return ring(q // 2, 2), part(ring(q, 2), B)
@@ -414,6 +422,9 @@
         for k in range(MS - 1):
             load_mid(k).start()
         if n == 0:
+            sums[...] = jnp.zeros_like(sums)
+            da[...] = jnp.zeros_like(da)
+            greet(r, y, z, c, device(r, 1 - y, z, 1 - c))
             load_dh.wait()
         else:
 
@@ -429,6 +440,15 @@
             load_h.wait()
             loop(T // N, norm)
 
+        def down_pieces(where, i):
+            if n:
+                for at, stages in STAGES[where]:
+                    when(i == at)(functools.partial(dr.run, stages, d_first))
+            elif where:
+                dr.tick(2 + where + 2 * i, d_first, DP)
+            else:
+                when((i == 4) | (i == 6) | (i == 9))(lambda: dr.tick((i - 4) // 2, d_first, DP))
+
         def tile(t, st, h):
             ddst[t] = tn(dgu[:, part(ring(st, MS), B)], dh[:, part(h, HALF)]).astype(bf16).reshape(ROWS, 8, HALF)
 
@@ -437,10 +457,8 @@
             def _():
                 load_mid(st + MS - 1).start()
 
-            @when(st == 1)
-            def _():
-                (load_a0 if n else load_a).start()
-                first_loads()
+            when(st == 4)(first_loads)
+            when(st == 6)((load_a0 if n else load_a).start)
 
             load_mid(st).wait()
             t, i, h = ring(st, 2), ring(st, NB), st // NB
@@ -456,15 +474,12 @@
             def _():
                 write_dd(i, h, t).wait()
 
-            @when((st == 4) | (st == 6) | (st == 9))
-            def _():
-                dr.tick((st - 4) // 2, d_first, DP)
+            down_pieces(0, st)
 
             if n:
 
-                @when((st == 0) | (st == 2) | (st == 5) | (st == 7) | (st == 9))
-                def _():
-                    gr.tick(GP + st // 2, 0, GP)
+                for i, at in enumerate((0, 4, 6, 8, 9)):
+                    when(st == at)(functools.partial(gr.tick, GP + i, 0, GP))
 
         loop(2 * NB, down)
         (load_a0 if n else load_a).wait()
@@ -493,7 +508,7 @@
             def _():
                 load_wd(j + 1).start()
 
-            dr.tick(3 + 2 * j, d_first, DP)
+            down_pieces(1, j)
 
             @when(j >= 1)
             def _():
@@ -504,7 +519,7 @@
 
             loop(D // R, terms)
 
-            dr.tick(4 + 2 * j, d_first, DP)
+            down_pieces(2, j)
             gr.tick(2 * j, g_first, GP)
 
             if n == 0:
@@ -524,20 +539,18 @@
         loop(NB, block)
         gr.tick(GP - 1, g_first, GP)
     loop(NB, lambda t: gr.tick(GP + t, GP, GP))
+    def swap(src, at, devs, sems):
+        copies = [remote(src, got.at[at], s_tot.at[send], s_tot_in.at[recv], dev) for (send, recv), dev in zip(sems, devs, strict=True)]
+        start(copies)
+        got[at] = src[...]
+        finish(copies)
+
+    swap(sums, y * 2 + c, (gr.partner, gr.across, device(r, 1 - y, z, 1 - c)), ((0, 0), (1, 1), (2, 2)))
+    tot[...] = got[0] + got[1] + got[2] + got[3]
+    swap(tot, 4 + z, gr.along, ((3, 5), (4, 4), (5, 3)))
+    sums_out[...] = got[4] + got[5] + got[6] + got[7]
     dr.close()
     gr.close()
-
-    tot[0] = sums[...]
-    for i, dev in enumerate((gr.partner, gr.across)):
-        copy = remote(tot.at[i], got.at[i], s_tot.at[i], s_tot_in.at[i], dev)
-        copy.start()
-        copy.wait()
-        tot[i + 1] = tot[i] + got[i]
-    copies = [remote(tot.at[2], got.at[2 + z], s_tot.at[2 + i], s_tot_in.at[4 - i], dev) for i, dev in enumerate(gr.along)]
-    start(copies)
-    finish(copies)
-    got[2 + z] = tot[2]
-    sums_out[...] = got[2] + got[3] + got[4] + got[5]
 
 
 def backward(*arrays):
@@ -555,7 +568,7 @@
             VMEM((8, 128), f32), VMEM((T, D), bf16), VMEM((T, D), bf16), VMEM((T, D), f32), VMEM((ES, R, B), f32), VMEM((ES, R, B), f32),
             VMEM((T, MS * B), bf16), VMEM((D, 2 * B), bf16), VMEM((B, D), bf16), VMEM((2, 8, 2, 64, 2 * B), bf16),
             VMEM((2, ROWS, 8, HALF), bf16), VMEM((DS[0], 8, 25, 8, DC), bf16),
-            VMEM((3, 8, 128), f32), VMEM((6, 8, 128), f32), DMA((5,)), DMA((5,)),
+            VMEM((8, 128), f32), VMEM((8, 8, 128), f32), DMA((6,)), DMA((6,)),
             DMA, DMA, DMA((ES, 2)), DMA((MS,)), DMA((2,)), DMA, DMA((2,)), DMA((DS[0], 8)),
         ] + Reducer.scratch((64, B), 1, GS) + Reducer.scratch((25, 8, DC), 8, DS),
         compiler_params=pltpu.CompilerParams(collective_id=0, has_side_effects=True, vmem_limit_bytes=67043328),
@@ -671,6 +684,24 @@
     return [o.reshape(2, -1, o.shape[-1]) for o in out]
 
 
+def settle_kernel(*refs):
+    sems = refs[-1]
+    copies = [pltpu.make_async_copy(src.at[layer], dst.at[layer], sems.at[i, layer]) for i, (src, dst) in enumerate(zip(refs[:3], refs[3:6], strict=True)) for layer in range(2)]
+    start(copies)
+    finish(copies)
+
+
+def settle(arrays):
+    return pl.pallas_call(
+        settle_kernel,
+        out_shape=[jax.ShapeDtypeStruct(a.shape, a.dtype) for a in arrays],
+        in_specs=[pl.BlockSpec(memory_space=pl.ANY)] * 3,
+        out_specs=[pl.BlockSpec(memory_space=HBM)] * 3,
+        scratch_shapes=[DMA((3, 2))],
+        compiler_params=pltpu.CompilerParams(vmem_limit_bytes=2**20),
+    )(*arrays)
+
+
 def adamw(w, m, v, g):
     m = 0.9 * m + 0.1 * g
     v = 0.95 * v + 0.05 * g * g
@@ -689,7 +720,7 @@
             rows = m.shape[1]
             mine = lax.dynamic_slice_in_dim(w, me * rows, rows, 1)
             new.append(adamw(mine.astype(f32), m, v, g.astype(f32) * factor))
-        weights = all_gather(*(n[0] for n in new))
+        weights = settle(all_gather(*(n[0] for n in new)))
         return (*weights, *(n[1] for n in new), *(n[2] for n in new))
 
     seq, rep, own = P(("rep", "dp")), P("rep"), P("rep", "dp")

time: 585 us -> 573 us (0.979)
  local copies, waits for them, and re-layouts: 14.8 us -> 0.01 us
    unnamed x3 -> x2, local copies, waits for them, and re-layouts: 14.8 us -> 0.01 us
    pallas_call x0 -> x1, Pallas kernels: none -> 12.9 us  [settle(): pl.pallas_call(settle_kernel, out_shape=[jax.ShapeDtypeStruct(a.shape, a....]
    pallas_call x1, Pallas kernels: 272 us -> 262 us  [backward(): pl.pallas_call(backward_kernel, out_shape=(jax.ShapeDtypeStruct((2, 2, 64...]
where the time goes in v5:
time: 573 us
  Pallas kernels  559 us (98%)
  other arithmetic  12.5 us (2%)
    pallas_call x1, Pallas kernels, backward(): pl.pallas_call(backward_kernel, out_shape=(jax.ShapeDtypeStruct((2, 2, 64...  262 us
    pallas_call x1, Pallas kernels, all_gather(): pl.pallas_call(gather_kernel, out_shape=[jax.ShapeDtypeStruct((2, 16, *s....  194 us
    pallas_call x1, Pallas kernels, forward(): pl.pallas_call(forward_kernel, out_shape=(states,) * 3 + (wide, wide, mid...  89.8 us
    pallas_call x1, Pallas kernels, settle(): pl.pallas_call(settle_kernel, out_shape=[jax.ShapeDtypeStruct(a.shape, a....  12.9 us

profile of v5, /device:TPU:0, one launch (start us, length us, event | category | flops | bytes accessed | tf_op | source)
XLA Modules:
  0.0 572.7 jit_solution(3192541488887450857)
XLA Ops:
  0.6 89.8 %shard_map.178 = (bf16[2048,1024]{1,0:T(8,128)(2,1)}, bf16[2048,1024]{1,0:T(8,128)(2,1)}, bf16[2048,1024]{1,0:T(8,128)(2,1)}, f32[2048,3200]{1,0:T(8,128)}, f32[...) custom-call(bf16[2048,1024]{1,0:T(8,128)(2,1)} %bitcast.30, ...), custom_call_target="tpu_custom_call" | custom-call | tf_op jit(solution)/shard_map/pallas_call | solution.py:167
  90.5 262.5 %shard_map.179 = (bf16[2,2,64,3200]{3,2,1,0:T(8,128)(2,1)}, bf16[2,25,8,1024]{3,2,1,0:T(8,128)(2,1)}, f32[8,128]{1,0:T(8,128)}, bf16[2,400,8,1024]{3,2,1,0:T(8,128)(2,1)}) custom-call(bf16[2048,1024]{1,0:T(8,128)(2,1)} %bitcast.29, bf16[2048,1024]{1,0:T(8,128)(2,1)} %get-tuple-element.27.h1_ref, bf16[2048,1024]{1,0:T(8,128)(2,1)} %get-tuple-element.28.a1_ref, ...), custom_call_target="tpu_custom_call" | custom-call | tf_op jit(solution)/shard_map/pallas_call | solution.py:557
  352.9 1.3 reduce_sum.9
  354.9 0.0 copy-start
  354.9 5.2 fusion.8
  360.2 0.0 copy-done
  360.2 5.9 %fusion.5 = (bf16[2,64,3200]{2,1,0:T(8,128)(2,1)S(1)}, f32[2,64,3200]{2,1,0:T(8,128)}, f32[2,64,3200]{2,1,0:T(8,128)}, bf16[2,64,3200]{2,1,0:T(8,128)(2,1)S(1)},...) fusion(bf16[2,1024,3200]{2,1,0:T(8,128)(2,1)} %wu_ref.3, s32[]{:T(128)S(6)} %select_n.7, f32[]{:T(128)S(6)} %min_shard_map.3, ...), kind=kLoop, calls=%fused_computation.14 | loop fusion | flops 13926400 | bytes 18022408 | tf_op jit(solution)/shard_map/convert_element_type | solution.py:709
  366.1 193.5 %shard_map.180 = (bf16[2,16,64,3200]{3,2,1,0:T(8,128)(2,1)S(1)}, bf16[2,16,64,3200]{3,2,1,0:T(8,128)(2,1)S(1)}, bf16[2,16,200,1024]{3,2,1,0:T(8,128)(2,1)S(1)}) custom-call(bf16[2,64,3200]{2,1,0:T(8,128)(2,1)S(1)} %get-tuple-element.54.sg, bf16[2,64,3200]{2,1,0:T(8,128)(2,1)S(1)} %get-tuple-element.48.su, bf16[2,200,1024]{2,1,0:T(8,128)(2,1)S(1)} %get-tuple-element.45.sd), custom_call_target="tpu_custom_call" | custom-call | tf_op jit(solution)/shard_map/pallas_call | solution.py:676
  559.6 12.9 %shard_map.181 = (bf16[2,1024,3200]{2,1,0:T(8,128)(2,1)}, bf16[2,1024,3200]{2,1,0:T(8,128)(2,1)}, bf16[2,3200,1024]{2,1,0:T(8,128)(2,1)}) custom-call(bf16[2,1024,3200]{2,1,0:T(8,128)(2,1)S(1)} %bitcast.26, bf16[2,1024,3200]{2,1,0:T(8,128)(2,1)S(1)} %bitcast.27, bf16[2,3200,1024]{2,1,0:T(8,128)(2,1)S(1)} %bitcast.28), custom_call_target="tpu_custom_call" | custom-call | tf_op jit(solution)/shard_map/pallas_call | solution.py:695
Async XLA Ops:
  354.9 5.2 copy-start
